TPU v7x, 32 devices: a whole 2x2x4 slice. The times are simulated.
32 devices in a mesh: req: 8 (over z, x), seq: 4 (over y, core).
Axes of the slice: x: 2, y: 2, z: 4, core: 2. Of those that a mesh axis runs over, the one named last changes fastest.
Arguments:
- pool_states: float32 [104, 64, 64, 128], P('req', 'seq'), may hold values from -6 to 6
- inner_window: bfloat16 [104, 3, 4096], P('req', None, 'seq'), may hold values from -6 to 6
- state_window: bfloat16 [104, 3, 256], P('req', None, 'seq'), may hold values from -6 to 6
- move_plan: int32 [104, 2], P('req'), may hold values from 0 to 12, as said below
- active_mask: int32 [104], P('req'), may hold values 0 or 1
- inputs_inner: bfloat16 [8, 2048, 4096], P('req', 'seq'), may hold values from -6 to 6
- inputs_state: bfloat16 [8, 2048, 256], P('req', 'seq'), may hold values from -6 to 6
- gate_rows: bfloat16 [8, 2048, 4096], P('req', 'seq'), may hold values from -6 to 6
- step_raw: bfloat16 [8, 2048, 64], P('req', 'seq'), may hold values from -8 to 60
- lengths: int32 [8], P('req'), may hold values from 4 to 2048
- conv_weight: float32 [4, 4352], replicated, may hold values from -3 to 3
- conv_bias: float32 [4352], replicated, may hold values from -3 to 3
- step_bias: float32 [64], replicated, may hold values from -3.3 to -2.7
- decay_log: float32 [64], replicated, may hold values from -10 to 0
- skip_weight: float32 [64], replicated, may hold values from 0.5 to 1.5
- norm_weight: float32 [4096], replicated, may hold values from 0.25 to 1.75
Outputs:
- new_states: float32 [104, 64, 64, 128], P('req', 'seq')
- new_inner_window: bfloat16 [104, 3, 4096], P('req', None, 'seq')
- new_state_window: bfloat16 [104, 3, 256], P('req', None, 'seq')
- mixer_out: bfloat16 [8, 2048, 4096], P('req', 'seq')
Inputs may be any that keep to these rules, and one draw needn't show every extreme that they name: `move_plan`: every pair of a destination index along req and a slot 0 .. 12 is named exactly once; the rows of one device name one destination at most 4 times, and some destination exactly 4 times.
All inputs are finite; a program needn't handle non-finite values. No bound on the sum of `active_mask` on one device may be relied on, other than what follows from the above.
Results may differ from a plain program's by a relative error of at most 0.0087.
Values may be sent and summed in bfloat16 or wider, within the bound.
A program may use at most 192 MiB of HBM per device.

v0:
```python
import functools

import jax
import jax.numpy as jnp
from jax import lax
from jax.experimental import pallas as pl
from jax.experimental.pallas import tpu as pltpu
from jax.sharding import PartitionSpec as P


HEAD_DIM = 64
STATE_DIM = 128
KERNEL = 4
BLOCK_LEN = 256
EPSILON = 1e-05
LANES = 128
HALO = 8
LOG2E = 1.4426950408889634
GROUP = 2 * LANES


def half_silu(v):
    return (0.5 * v) * (1.0 + jnp.tanh(0.5 * v))


def conv_rows(ext_ref, weight_ref, bias_ref, start, count):
    total = bias_ref[...] + weight_ref[KERNEL - 1 : KERNEL, :] * ext_ref[pl.ds(start + HALO, count), :]
    for k in range(KERNEL - 1):
        total = total + weight_ref[k : k + 1, :] * ext_ref[pl.ds(start + HALO - KERNEL + 1 + k, count), :]
    return half_silu(total).astype(jnp.bfloat16)


def mix_kernel(
    nv_ref, x_ref, win_ref, cw_ref, cb_ref, skip_ref, xs_ref, wins_ref, cws_ref, cbs_ref, step_ref, sbias_ref, dlog_ref,
    part_ref, end_ref, ecum_ref, read_ref,
    ext, val, a_s, te_s, brow, write_t, score,
):
    g = pl.program_id(0)
    length = x_ref.shape[0]
    blocks = length // BLOCK_LEN
    half = BLOCK_LEN // 2

    @pl.when(g == 0)
    def _():
        ext[0:HALO, :] = wins_ref[...].astype(jnp.float32)
        ext[HALO : HALO + length, :] = xs_ref[...].astype(jnp.float32)
        ys = conv_rows(ext, cws_ref, cbs_ref, 0, length)
        write, read = ys[:, :STATE_DIM], ys[:, STATE_DIM:]
        read_ref[...] = read
        write_t[...] = write.astype(jnp.float32).T.astype(jnp.bfloat16)
        rows = lax.broadcasted_iota(jnp.int32, (length, LANES), 0)
        raw = step_ref[...] + sbias_ref[...]
        soft = jnp.maximum(raw, 0.0) + jnp.log1p(jnp.exp(-jnp.abs(raw)))
        dt = jnp.where(rows < nv_ref[0], soft, 0.0)
        rate = (dt * LOG2E) * (-jnp.exp(dlog_ref[...]))
        r = lax.broadcasted_iota(jnp.int32, (BLOCK_LEN, BLOCK_LEN), 0)
        c = lax.broadcasted_iota(jnp.int32, (BLOCK_LEN, BLOCK_LEN), 1)
        tri = (r >= c).astype(jnp.float32)
        before = jnp.zeros((1, LANES), jnp.float32)
        for blk in range(blocks):
            s = slice(blk * BLOCK_LEN, (blk + 1) * BLOCK_LEN)
            cum = jnp.dot(tri, rate[s], precision=lax.Precision.HIGHEST, preferred_element_type=jnp.float32)
            b = jnp.where(dt[s] > 0.0, cum - jnp.log2(dt[s]), 1e30)
            a_s[s, :] = cum
            last = cum[BLOCK_LEN - 1 : BLOCK_LEN, :]
            te_s[s, :] = jnp.exp2(last - b)
            brow[:, s] = b.T
            ecum_ref[s, :] = jnp.exp2(cum + before)
            before = before + last
            sc = lax.dot_general(read[s], write[s], (((1,), (1,)), ((), ())), preferred_element_type=jnp.float32)
            score[blk] = jnp.where(r >= c, sc, 0.0)

    ext[0:HALO, :] = win_ref[...].astype(jnp.float32)
    ext[HALO : HALO + length, :] = x_ref[...].astype(jnp.float32)
    rows_at_once = 64
    for i in range(length // rows_at_once):
        val[i * rows_at_once : (i + 1) * rows_at_once, :] = conv_rows(ext, cw_ref, cb_ref, i * rows_at_once, rows_at_once)

    heads_step = GROUP // HEAD_DIM
    turn = lax.rem(LANES - heads_step * g, LANES)
    a_all = pltpu.roll(a_s[...], turn, axis=1)
    te_all = pltpu.roll(te_s[...], turn, axis=1)
    low = lax.broadcasted_iota(jnp.int32, (1, LANES), 1) < HEAD_DIM

    for pair in range(GROUP // LANES):
        cols = slice(pair * LANES, (pair + 1) * LANES)
        skip = skip_ref[:, cols]
        before = None
        for blk in range(blocks):
            s = slice(blk * BLOCK_LEN, (blk + 1) * BLOCK_LEN)
            v = val[s, cols]
            vf = v.astype(jnp.float32)
            masked = [jnp.where(low, vf, 0.0).astype(jnp.bfloat16), jnp.where(low, 0.0, vf).astype(jnp.bfloat16)]
            tops, bottoms = [], []
            for j in range(2):
                h = 2 * pair + j
                a = a_all[s, h : h + 1]
                b = brow[pl.ds(heads_step * g + h, 1), s]
                top = jnp.exp2(jnp.minimum(a[:half] - b[:, :half], 126.0)) * score[blk, :half, :half]
                bot = jnp.exp2(jnp.minimum(a[half:] - b, 126.0)) * score[blk, half:, :]
                tops.append(top.astype(jnp.bfloat16))
                bottoms.append(bot.astype(jnp.bfloat16))
            intra_top = jnp.dot(
                jnp.concatenate(tops, axis=1), jnp.concatenate([m[:half] for m in masked], axis=0), preferred_element_type=jnp.float32
            )
            intra_bot = jnp.dot(
                jnp.concatenate(bottoms, axis=1), jnp.concatenate(masked, axis=0), preferred_element_type=jnp.float32
            )
            out = jnp.concatenate([intra_top, intra_bot], axis=0) + skip * vf
            h = 2 * pair
            te = jnp.where(low, te_all[s, h : h + 1], te_all[s, h + 1 : h + 2])
            state = jnp.dot(write_t[:, s], (te * vf).astype(jnp.bfloat16), preferred_element_type=jnp.float32)
            if blk > 0:
                e = jnp.exp2(jnp.where(low, a_all[s, h : h + 1], a_all[s, h + 1 : h + 2]))
                out = out + e * jnp.dot(read_ref[s, :], before.astype(jnp.bfloat16), preferred_element_type=jnp.float32)
                state = state + e[BLOCK_LEN - 1 : BLOCK_LEN, :] * before
            before = state
            part_ref[s, cols] = out.astype(jnp.bfloat16)
        end_ref[:, cols] = before.astype(jnp.bfloat16)


def mix(nv, x, xs, window, conv_weight, conv_bias, step_raw, step_bias, decay_log, skip_row):
    length, inner = x.shape
    pad = LANES - step_raw.shape[1]
    step = jnp.pad(step_raw.astype(jnp.float32), ((0, 0), (0, pad)))
    sbias = jnp.pad(step_bias, (0, pad))[None]
    dlog = jnp.pad(decay_log, (0, pad))[None]
    xs_width = xs.shape[1]
    beyond = inner // xs_width
    state_column = lambda rows: pl.BlockSpec((rows, xs_width), lambda i, nv: (0, beyond))
    fixed = lambda shape: pl.BlockSpec(shape, lambda i, nv: (0,) * len(shape))
    column = lambda rows: pl.BlockSpec((rows, GROUP), lambda i, nv: (0, i))
    blocks = length // BLOCK_LEN
    heads = inner // HEAD_DIM
    return pl.pallas_call(
        mix_kernel,
        grid_spec=pltpu.PrefetchScalarGridSpec(
            num_scalar_prefetch=1,
            grid=(inner // GROUP,),
            in_specs=[
                column(length), column(HALO), column(KERNEL), column(1), column(1),
                fixed((length, xs_width)), state_column(HALO), state_column(KERNEL), state_column(1),
                fixed((length, LANES)), fixed((1, LANES)), fixed((1, LANES)),
            ],
            out_specs=[column(length), column(STATE_DIM), fixed((length, LANES)), fixed((length, STATE_DIM))],
            scratch_shapes=[
                pltpu.VMEM((length + HALO, GROUP), jnp.float32),
                pltpu.VMEM((length, GROUP), jnp.bfloat16),
                pltpu.VMEM((length, LANES), jnp.float32),
                pltpu.VMEM((length, LANES), jnp.float32),
                pltpu.VMEM((LANES, length), jnp.float32),
                pltpu.VMEM((STATE_DIM, length), jnp.bfloat16),
                pltpu.VMEM((blocks, BLOCK_LEN, BLOCK_LEN), jnp.float32),
            ],
        ),
        out_shape=[
            jax.ShapeDtypeStruct((length, inner), jnp.bfloat16),
            jax.ShapeDtypeStruct((STATE_DIM, inner), jnp.bfloat16),
            jax.ShapeDtypeStruct((length, LANES), jnp.float32),
            jax.ShapeDtypeStruct((length, STATE_DIM), jnp.bfloat16),
        ],
        compiler_params=pltpu.CompilerParams(dimension_semantics=("arbitrary",)),
        cost_estimate=pl.CostEstimate(
            flops=2 * blocks * heads * BLOCK_LEN * BLOCK_LEN * LANES * 8,
            bytes_accessed=4 * length * inner, transcendentals=blocks * heads * BLOCK_LEN * BLOCK_LEN,
        ),
        name="mix",
    )(
        nv, x, window, conv_weight, conv_bias[None], skip_row, xs, window, conv_weight, conv_bias[None], step, sbias, dlog,
    )


CHUNK = 256


def finish_kernel(
    nv_ref, part_ref, gate_ref, read_ref, ecum_ref, coef_ref, init_ref, norm_ref, *refs
):
    out_ref, token_ref, prior, spread, gated = refs[-5:]
    ends_refs = refs[:-5]
    token_ref[0] = 0
    step = pl.program_id(0)
    tile, inner = part_ref.shape
    links = len(ends_refs)
    own_width = init_ref.shape[1]
    heads = inner // HEAD_DIM

    @pl.when(step == 0)
    def _():
        def fill(i, carry):
            cols = pl.ds(pl.multiple_of(i * CHUNK, CHUNK), CHUNK)
            total = coef_ref[0:1, cols] * ends_refs[0][:, cols].astype(jnp.float32)
            for j in range(1, links):
                total = total + coef_ref[j : j + 1, cols] * ends_refs[j][:, cols].astype(jnp.float32)
            prior[:, cols] = total.astype(jnp.bfloat16)
            k = lax.broadcasted_iota(jnp.int32, (LANES, CHUNK), 0)
            c = lax.broadcasted_iota(jnp.int32, (LANES, CHUNK), 1)
            owner = i * (CHUNK // HEAD_DIM) + c // HEAD_DIM
            spread[:, cols] = jnp.where((k == owner) | (k == owner + heads), 1.0, 0.0).astype(jnp.bfloat16)
            return carry

        lax.fori_loop(0, inner // CHUNK, fill, 0)

    read = read_ref[...]
    ecum = ecum_ref[...]
    first = ecum.astype(jnp.bfloat16).astype(jnp.float32)
    lane = lax.broadcasted_iota(jnp.int32, (tile, LANES), 1)
    both = jnp.where(lane < heads, first, pltpu.roll(ecum - first, heads, axis=1)).astype(jnp.bfloat16)
    rows = lax.broadcasted_iota(jnp.int32, (tile, 1), 0) + step * tile
    valid = (rows < nv_ref[0]).astype(jnp.float32)

    def gate_chunk(i, squares):
        cols = pl.ds(pl.multiple_of(i * CHUNK, CHUNK), CHUNK)
        z = jnp.dot(read, prior[:, cols], preferred_element_type=jnp.float32)
        chunks = own_width // CHUNK
        turned = nv_ref[1] ^ (i // chunks)
        own = init_ref[turned, pl.ds(pl.multiple_of(lax.rem(i, chunks) * CHUNK, CHUNK), CHUNK), :]
        zi = lax.dot_general(read, own, (((1,), (1,)), ((), ())), preferred_element_type=jnp.float32)
        e = jnp.dot(both, spread[:, cols], preferred_element_type=jnp.float32)
        z = z + coef_ref[links : links + 1, cols] * zi
        y = (part_ref[:, cols].astype(jnp.float32) + e * z) * valid
        y = y.astype(jnp.bfloat16).astype(jnp.float32)
        out = y * half_silu(gate_ref[:, cols].astype(jnp.float32))
        gated[:, cols] = out
        square = out * out
        for k in range(CHUNK // LANES):
            squares = squares + square[:, k * LANES : (k + 1) * LANES]
        return squares

    squares = lax.fori_loop(0, inner // CHUNK, gate_chunk, jnp.zeros((tile, LANES), jnp.float32), unroll=2)
    scale = lax.rsqrt(jnp.sum(squares, axis=1, keepdims=True) * (1.0 / inner) + EPSILON)

    def scale_chunk(i, carry):
        cols = pl.ds(pl.multiple_of(i * CHUNK, CHUNK), CHUNK)
        out_ref[:, cols] = (gated[:, cols] * scale * norm_ref[:, cols]).astype(jnp.bfloat16)
        return carry

    lax.fori_loop(0, inner // CHUNK, scale_chunk, 0, unroll=2)


def finish(nv, part, gate, read, ecum, ends, coef, initial, norm):
    length, inner = part.shape
    tile = min(128, length)
    fixed = lambda shape: pl.BlockSpec(shape, lambda i, nv: (0,) * len(shape))
    row = lambda width: pl.BlockSpec((tile, width), lambda i, nv: (i, 0))
    return pl.pallas_call(
        finish_kernel,
        grid_spec=pltpu.PrefetchScalarGridSpec(
            num_scalar_prefetch=1,
            grid=(length // tile,),
            in_specs=[
                row(inner), row(inner), row(STATE_DIM), row(LANES),
                fixed(coef.shape), fixed(initial.shape), fixed((1, inner)), *[fixed(e.shape) for e in ends],
            ],
            out_specs=[row(inner), pl.BlockSpec(memory_space=pltpu.SMEM)],
            scratch_shapes=[
                pltpu.VMEM((STATE_DIM, inner), jnp.bfloat16),
                pltpu.VMEM((LANES, inner), jnp.bfloat16),
                pltpu.VMEM((tile, inner), jnp.float32),
            ],
        ),
        out_shape=[jax.ShapeDtypeStruct((length, inner), jnp.bfloat16), jax.ShapeDtypeStruct((1,), jnp.int32)],
        compiler_params=pltpu.CompilerParams(dimension_semantics=("arbitrary",)),
        cost_estimate=pl.CostEstimate(
            flops=40 * length * inner * STATE_DIM // 8, bytes_accessed=6 * length * inner, transcendentals=length * inner
        ),
        name="finish",
    )(nv, part, gate, read, ecum, coef, initial, norm, *ends)


def pack_kernel(keep_ref, state_ref, out_ref, held, packed, in_sem, out_sem):
    peers, slots, rows, _ = out_ref.shape

    def load(j):
        return pltpu.make_async_copy(state_ref.at[j], held.at[j], in_sem.at[j])

    def store(j):
        return pltpu.make_async_copy(packed.at[j], out_ref.at[:, j], out_sem.at[j])

    def first(j, carry):
        load(j).start()
        return carry

    def second(j, carry):
        load(j).wait()
        keep = keep_ref[j].astype(jnp.float32)
        for i in range(peers):
            packed[j, i] = (held[j, i * rows : (i + 1) * rows] * keep).astype(packed.dtype)
        store(j).start()
        return carry

    def third(j, carry):
        store(j).wait()
        return carry

    lax.fori_loop(0, slots, first, 0)
    lax.fori_loop(0, slots, second, 0)
    lax.fori_loop(0, slots, third, 0)


def pack_pieces(states, keep, peers):
    slots, rows, lanes = states.shape
    piece = rows // peers
    return pl.pallas_call(
        pack_kernel,
        in_specs=[pl.BlockSpec(memory_space=pltpu.SMEM), pl.BlockSpec(memory_space=pl.ANY)],
        out_specs=pl.BlockSpec(memory_space=pl.ANY),
        out_shape=jax.ShapeDtypeStruct((peers, slots, piece, lanes), jnp.bfloat16),
        scratch_shapes=[
            pltpu.VMEM((slots, rows, lanes), jnp.float32),
            pltpu.VMEM((slots, peers, piece, lanes), jnp.bfloat16),
            pltpu.SemaphoreType.DMA((slots,)),
            pltpu.SemaphoreType.DMA((slots,)),
        ],
        cost_estimate=pl.CostEstimate(flops=20 * slots * rows * lanes, bytes_accessed=6 * slots * rows * lanes, transcendentals=0),
        name="pack",
    )(keep, states)


def letters_kernel(capacity, plan_ref, mask_ref, inner_ref, outer_ref, plan_row_ref, out_ref, table, count, wide_inner, wide_outer):
    taps, slots, inner = inner_ref.shape
    outer = outer_ref.shape[2]
    peers, rows, width = out_ref.shape
    wide_inner[...] = inner_ref[...].astype(jnp.float32)
    wide_outer[...] = outer_ref[...].astype(jnp.float32)

    def clear(d, carry):
        count[d] = 0
        for r in range(capacity):
            table[d * capacity + r] = -1
        return carry

    def enter(j, carry):
        d = plan_ref[0, j]
        table[d * capacity + count[d]] = jnp.where(mask_ref[j] != 0, j, -1)
        count[d] = count[d] + 1
        return carry

    lax.fori_loop(0, peers, clear, 0)
    lax.fori_loop(0, slots, enter, 0)

    def fill(d, carry):
        pieces = []
        for r in range(capacity):
            j = table[d * capacity + r]
            at = jnp.maximum(j, 0)
            for t in range(taps):
                row = jnp.concatenate(
                    [wide_inner[t, pl.ds(at, 1), :], wide_outer[t, pl.ds(at, 1), :], jnp.zeros((1, width - inner - outer), jnp.float32)],
                    axis=1,
                )
                pieces.append(jnp.where(j >= 0, row, 0.0))
        pieces.append(plan_row_ref[...])
        left = rows - taps * capacity - 1
        if left:
            pieces.append(jnp.zeros((left, width), jnp.float32))
        out_ref[d] = jnp.concatenate(pieces, axis=0).astype(out_ref.dtype)
        return carry

    lax.fori_loop(0, peers, fill, 0)


def letters(plan, mask, inner_window, outer_window, peers, capacity):
    slots, taps, inner = inner_window.shape
    outer = outer_window.shape[2]
    width = inner + outer
    width += -width % LANES
    rows = taps * capacity + 1
    rows += -rows % 16
    plan_row = jnp.concatenate([plan[:, 0], plan[:, 1], mask]).astype(jnp.float32)[None]
    plan_row = jnp.pad(plan_row, ((0, 0), (0, width - 3 * slots)))
    smem, vmem = pl.BlockSpec(memory_space=pltpu.SMEM), pl.BlockSpec(memory_space=pltpu.VMEM)
    return pl.pallas_call(
        functools.partial(letters_kernel, capacity),
        in_specs=[smem, smem, vmem, vmem, vmem],
        out_specs=vmem,
        out_shape=jax.ShapeDtypeStruct((peers, rows, width), jnp.bfloat16),
        scratch_shapes=[
            pltpu.SMEM((peers * capacity,), jnp.int32),
            pltpu.SMEM((peers,), jnp.int32),
            pltpu.VMEM((taps, slots, inner), jnp.float32),
            pltpu.VMEM((taps, slots, outer), jnp.float32),
        ],
        cost_estimate=pl.CostEstimate(flops=100000, bytes_accessed=8 * slots * taps * width, transcendentals=0),
        name="letters",
    )(plan.T, mask, jnp.moveaxis(inner_window, 1, 0), jnp.moveaxis(outer_window, 1, 0), plan_row)


def sort_kernel(table_ref, got_ref, *refs):
    stage, in_sem, out_sem = refs[-3:]
    outs, token_ref = refs[:-4], refs[-4]
    parts, count = stage.shape[:2]
    token_ref[0] = 0

    def one(k, carry):
        for m in range(parts):
            pltpu.make_async_copy(got_ref.at[table_ref[m, k]], stage.at[m, k], in_sem.at[m]).start()
        return carry

    lax.fori_loop(0, count, one, 0)
    copies = [pltpu.make_async_copy(stage.at[m], outs[m], out_sem.at[m]) for m in range(parts)]
    for m in range(parts):
        pltpu.make_async_copy(got_ref.at[0:count], stage.at[m], in_sem.at[m]).wait()
        copies[m].start()
    for copy in copies:
        copy.wait()


def sort_pieces(table, got, count):
    parts = table.shape[0]
    rows, lanes = got.shape[1:]
    smem, whole = pl.BlockSpec(memory_space=pltpu.SMEM), pl.BlockSpec(memory_space=pl.ANY)
    *outs, token = pl.pallas_call(
        sort_kernel,
        in_specs=[smem, whole],
        out_specs=[whole] * parts + [smem],
        out_shape=[jax.ShapeDtypeStruct((count, rows, lanes), jnp.bfloat16)] * parts + [jax.ShapeDtypeStruct((1,), jnp.int32)],
        scratch_shapes=[
            pltpu.VMEM((parts, count, rows, lanes), jnp.bfloat16),
            pltpu.SemaphoreType.DMA((parts,)),
            pltpu.SemaphoreType.DMA((parts,)),
        ],
        cost_estimate=pl.CostEstimate(flops=10 * parts * count * rows * lanes, bytes_accessed=4 * parts * count * rows * lanes, transcendentals=0),
        name="sort",
    )(table, got)
    return outs, token[0]


def tables_kernel(peers, parts, slots, capacity, place_ref, plan_ref, near_ref, far_ref, first_ref, info_ref, box_ref, need_ref, inverse):
    me, side, seat = place_ref[0], place_ref[1], place_ref[2]

    def one_source(r, carry):
        def one_slot(j, count):
            d, k = plan_ref[r, j], plan_ref[r, slots + j]
            inverse[d * slots + k] = (r << 9) + (j << 1) + plan_ref[r, 2 * slots + j]

            @pl.when(d == me)
            def _():
                box_ref[k] = r * capacity + count

            return count + (d == me).astype(jnp.int32)

        lax.fori_loop(0, slots, one_slot, 0)
        return carry

    def clear(k, carry):
        for m in range(parts):
            near_ref[m, k] = 0
            far_ref[m, k] = 0
        return carry

    lax.fori_loop(0, peers, one_source, 0)
    lax.fori_loop(0, slots - 1, clear, 0)

    def one_target(d, most):
        d_side = (d >= parts).astype(jnp.int32)
        m = lax.rem(d - d_side * parts + parts - seat, parts)

        def one_slot(k, count):
            code = inverse[d * slots + k]
            live = (code & 1) == 1
            r = code >> 9
            r_side = (r >= parts).astype(jnp.int32)
            held = (r - r_side * parts) * slots + ((code >> 1) & 255)
            far = live & (r_side != d_side)

            @pl.when(d == me)
            def _():
                info_ref[0, k] = jnp.where(live, jnp.where(far, 2, 1), 0)
                info_ref[1, k] = count
                info_ref[2, k] = seat

            @pl.when(k == 0)
            def _():
                first_ref[0, d] = jnp.where(live & (r_side == side), held, 0)

            @pl.when(live & (k > 0) & (r_side == side) & (d_side == side))
            def _():
                near_ref[m, k - 1] = held

            @pl.when(far & (k > 0) & (r_side == side))
            def _():
                far_ref[m, count] = held

            return count + (far & (k > 0)).astype(jnp.int32)

        return jnp.maximum(most, lax.fori_loop(0, slots, one_slot, 0))

    need_ref[0] = lax.fori_loop(0, peers, one_target, 0)


def tables(place, plan, peers, parts, slots, capacity):
    smem = pl.BlockSpec(memory_space=pltpu.SMEM)
    ints = lambda *shape: jax.ShapeDtypeStruct(shape, jnp.int32)
    return pl.pallas_call(
        functools.partial(tables_kernel, peers, parts, slots, capacity),
        in_specs=[smem, smem],
        out_specs=[smem] * 6,
        out_shape=[ints(parts, slots - 1), ints(parts, slots - 1), ints(1, peers), ints(3, slots), ints(slots), ints(1)],
        scratch_shapes=[pltpu.SMEM((peers * slots,), jnp.int32)],
        cost_estimate=pl.CostEstimate(flops=1000000, bytes_accessed=4000, transcendentals=0),
        name="tables",
    )(place, plan)


def land_kernel(parts, info_ref, final_ref, whole_ref, initial_ref, *refs):
    near, far = refs[:parts], refs[parts : 2 * parts]
    out_ref, held, wide, in_sem, out_sem = refs[2 * parts :]
    rest, rows, _ = near[0].shape
    slots = rest + 1

    def each(k, act):
        kind, at = info_ref[0, k], info_ref[1, k]
        for m in range(parts):

            @pl.when(kind == 1)
            def _():
                act(pltpu.make_async_copy(near[m].at[k - 1], held.at[k, m], in_sem.at[k]))

            @pl.when(kind == 2)
            def _():
                act(pltpu.make_async_copy(far[m].at[at], held.at[k, m], in_sem.at[k]))

    def store(k):
        return pltpu.make_async_copy(wide.at[k], out_ref.at[k], out_sem.at[k])

    def first(k, carry):
        each(k, lambda copy: copy.start())
        return carry

    def second(k, carry):
        each(k, lambda copy: copy.wait())
        kind = info_ref[0, k]
        for m in range(parts):
            begin = pl.multiple_of(lax.rem(info_ref[2, 1] + parts - m, parts) * rows, rows)
            wide[k, pl.ds(begin, rows)] = jnp.where(kind > 0, held[k, m].astype(wide.dtype), 0.0)
        store(k).start()
        return carry

    def third(k, carry):
        store(k).wait()
        return carry

    lax.fori_loop(1, slots, first, 0)
    for i in range(0, final_ref.shape[1], LANES):
        own = slice(i, i + LANES)
        moved = initial_ref[own, :].astype(jnp.float32).T
        wide[0, own, :] = (final_ref[:, own] + whole_ref[:, own] * moved).T
    store(0).start()
    lax.fori_loop(1, slots, second, 0)
    lax.fori_loop(0, slots, third, 0)


def land(info, final, whole_own, initial_own, near, far):
    parts = len(near)
    rest, rows, lanes = near[0].shape
    slots = rest + 1
    smem, vmem, whole = (pl.BlockSpec(memory_space=space) for space in (pltpu.SMEM, pltpu.VMEM, pl.ANY))
    return pl.pallas_call(
        functools.partial(land_kernel, parts),
        in_specs=[smem, vmem, vmem, vmem] + [whole] * (2 * parts),
        out_specs=whole,
        out_shape=jax.ShapeDtypeStruct((slots, parts * rows, lanes), jnp.float32),
        scratch_shapes=[
            pltpu.VMEM((slots, parts, rows, lanes), jnp.bfloat16),
            pltpu.VMEM((slots, parts * rows, lanes), jnp.float32),
            pltpu.SemaphoreType.DMA((slots,)),
            pltpu.SemaphoreType.DMA((slots,)),
        ],
        cost_estimate=pl.CostEstimate(
            flops=20 * slots * parts * rows * lanes, bytes_accessed=6 * slots * parts * rows * lanes, transcendentals=0
        ),
        name="land",
    )(info, final, whole_own, initial_own, *near, *far)


def exchange(source):
    return lax.all_to_all(source, "req", split_axis=0, concat_axis=0, tiled=True)


def flip(value, axis, step):
    return lax.ppermute(value, axis, [(r, r ^ step) for r in range(lax.axis_size(axis))])


def by_mask(value, axis):
    held, step = {0: value}, lax.axis_size(axis) // 2
    while step:
        masks = sorted(held)
        came = flip(jnp.stack([held[m] for m in masks]) if len(masks) > 1 else held[masks[0]][None], axis, step)
        held.update({m ^ step: came[i] for i, m in enumerate(masks)})
        step //= 2
    return [held[m] for m in sorted(held)]


LIMITS = (7, 9)


def on_device(
    pool_states, inner_window, state_window, move_plan, active_mask, inputs_inner, inputs_state, gate_rows, step_raw,
    lengths, conv_weight, conv_bias, step_bias, decay_log, skip_weight, norm_weight,
):
    peers, me = lax.axis_size("req"), lax.axis_index("req")
    chain, rank = lax.axis_size("seq"), lax.axis_index("seq")
    slots, _ = pool_states.shape[:2]
    length, inner = inputs_inner.shape[1:]
    own_width = inner_window.shape[2]
    states = pool_states.reshape(slots, -1, pool_states.shape[-1])
    rows = states.shape[1]

    capacity = (2 * slots + peers - 1) // peers
    index = jnp.arange(slots, dtype=jnp.int32)
    sides = 2
    parts = peers // sides
    side, seat = me // parts, lax.rem(me, parts)
    every = exchange(letters(move_plan, active_mask, inner_window, state_window, peers, capacity))
    packed = pack_pieces(states, active_mask, parts)
    packed, every = lax.optimization_barrier((packed, every))
    groups = [list(range(z * parts, (z + 1) * parts)) for z in range(sides)]
    got = lax.all_to_all(packed, "req", 0, 0, axis_index_groups=groups, tiled=True)
    got = got.reshape((parts * slots,) + got.shape[2:])

    def hop(value, across, by):
        pairs = [
            (z * parts + q, ((z + across) % sides) * parts + (q + by) % parts) for z in range(sides) for q in range(parts)
        ]
        return lax.ppermute(value, "req", pairs)

    taps = KERNEL - 1
    outer_own = state_window.shape[2]
    every_plan = every[:, taps * capacity, : 3 * slots].astype(jnp.int32)
    x, xs = inputs_inner[0], inputs_state[0]
    tail = jnp.concatenate([x[length - taps :], xs[length - taps :]], axis=1)
    to_me = every_plan[:, :slots] == me
    wanted = to_me & (every_plan[:, slots : 2 * slots] == 0)
    head_rank = jnp.sum(jnp.where(to_me & (index < jnp.sum(jnp.where(wanted, index, 0))), 1, 0) * jnp.any(wanted, axis=1, keepdims=True))
    head_peer = jnp.sum(jnp.where(wanted, jnp.arange(peers, dtype=jnp.int32)[:, None], 0))
    head_boxes = lax.dynamic_index_in_dim(every, head_peer, 0, keepdims=False)
    head = lax.dynamic_slice_in_dim(head_boxes, head_rank * taps, taps, 0)[:, : own_width + outer_own]

    positions = rank * length + jnp.arange(length, dtype=jnp.int32)
    steps = jax.nn.softplus(step_raw[0].astype(jnp.float32) + step_bias) * (positions < lengths[0])[:, None]
    own_decay = jnp.exp(jnp.sum(steps * -jnp.exp(decay_log), axis=0))
    digits, left = [], own_decay
    for _ in range(taps):
        digits.append(left.astype(jnp.bfloat16))
        left = left - digits[-1].astype(jnp.float32)
    edges = lax.all_gather(jnp.concatenate([tail, head, jnp.stack(digits)], axis=1), "seq")
    decays = jnp.sum(edges[:, :, tail.shape[1] + head.shape[1] :].astype(jnp.float32), axis=1)
    near_table, far_table, first_table, info, own_box, needed = tables(
        jnp.stack([me, side, seat]).astype(jnp.int32), every_plan, peers, parts, slots, capacity
    )
    before = lax.dynamic_index_in_dim(edges, lax.rem(rank + chain - 1, chain), 0, keepdims=False)[:, : tail.shape[1]]
    head = edges[:, :, tail.shape[1] : tail.shape[1] + head.shape[1]]
    head_inner = jnp.moveaxis(head[:, :, :own_width], 0, 1).reshape(taps, -1)
    head_outer = jnp.moveaxis(head[:, :, own_width:], 0, 1).reshape(taps, -1)
    window = jnp.where(rank == 0, jnp.concatenate([head_inner, head_outer], axis=1), before)
    window = jnp.pad(window.astype(jnp.float32), ((HALO - taps, 0), (0, 0)))

    valid_count = (lengths - rank * length).astype(jnp.int32)
    skip_row = jnp.repeat(skip_weight, HEAD_DIM)[None]
    seqs = jnp.arange(chain)
    coef, second_rows = [], []
    group = jnp.ones_like(decays[0])
    step = 1
    while step < chain:
        upper = (rank // step) % 2
        base = (rank // (2 * step)) * (2 * step)
        second = (seqs >= base + step) & (seqs < base + 2 * step)
        first_half = (seqs >= base) & (seqs < base + step)
        second_rows.append(jnp.prod(jnp.where(second[:, None], decays, 1.0), axis=0))
        coef.append(jnp.where(upper == 1, group, 0.0))
        group = jnp.where(upper == 1, group * jnp.prod(jnp.where(first_half[:, None], decays, 1.0), axis=0), group)
        step *= 2
    levels = len(coef)
    factors = jnp.repeat(jnp.stack(coef + [group] + second_rows + [jnp.prod(decays, axis=0)]), HEAD_DIM, axis=1)
    whole_own = lax.dynamic_slice_in_dim(factors[2 * levels + 1 :], rank * own_width, own_width, 1)

    def arrive(
        limit, got, first_table, near_table, far_table, info, own_box, every, x, xs, window, factors, whole_own, valid_count,
        conv_weight, conv_bias, step_raw, skip_row, gate, norm,
    ):
        first, token = sort_pieces(first_table, got, peers)
        first = exchange(first[0])
        far_all, token = sort_pieces(far_table + token, got, limit)
        far = [hop(far_all[m], 1, m) for m in range(parts)]
        near_all, token = sort_pieces(near_table + token, got, slots - 1)
        near = [near_all[0]] + [hop(near_all[m], 0, m) for m in range(1, parts)]
        part, end, ecum, read = mix(
            valid_count + token, x, xs, window, conv_weight, conv_bias, step_raw, step_bias, decay_log, skip_row
        )
        ends, total = [], end
        step = 1
        for level in range(levels):
            if level == 1:
                odd, width = rank % 2, inner // 2
                part_came = flip(lax.dynamic_slice_in_dim(total, odd * width, width, 1), "seq", step)
                part_other = flip(part_came, "seq", 1)
                came_end = jnp.concatenate(
                    [jnp.where(odd == 0, part_came, part_other), jnp.where(odd == 0, part_other, part_came)], axis=1
                )
            else:
                came_end = flip(total, "seq", step)
            upper = (rank // step) % 2
            ends.append(came_end)
            row = factors[levels + 1 + level][None]
            low, high = jnp.where(upper == 1, came_end, total), jnp.where(upper == 1, total, came_end)
            step *= 2
            if step < chain:
                total = (row * low.astype(jnp.float32) + high.astype(jnp.float32)).astype(jnp.bfloat16)
            else:
                own = lambda array: lax.dynamic_slice_in_dim(array, rank * own_width, own_width, 1)
                final = own(row) * own(low).astype(jnp.float32) + own(high).astype(jnp.float32)
        after = (total[0, 0].astype(jnp.float32) * 0.0).astype(jnp.int32)
        kind = info[0, 0]
        initial_own = lax.dynamic_slice_in_dim(first, jnp.where(kind == 1, side, 1 - side) * parts, parts, 0).reshape(rows, -1)
        initial_own = jnp.where(kind > 0, initial_own, jnp.zeros_like(initial_own))
        initial = jnp.stack(by_mask(initial_own, "seq"))
        out, token = finish(
            jnp.concatenate([valid_count, rank[None]]), part, gate, read, ecum, ends, factors, initial, norm
        )
        placed = land(info, final, whole_own, initial_own, near, far)
        position = lengths[0] + after - taps + jnp.arange(taps, dtype=jnp.int32) - rank * length
        inside = (position >= 0) & (position < length)
        clipped = jnp.clip(position, 0, length - 1)
        last = jnp.concatenate([jnp.take(x, clipped, axis=0), jnp.take(xs, clipped, axis=0)], axis=1)
        last = jnp.where(inside[:, None], last, jnp.zeros_like(last))
        kept = sum(piece.astype(jnp.float32) for piece in by_mask(last, "seq")).astype(jnp.bfloat16)
        kept_inner = lax.dynamic_slice_in_dim(kept, rank * own_width, own_width, 1)
        kept_outer = lax.dynamic_slice_in_dim(kept, inner + rank * outer_own, outer_own, 1)
        came = every[:, : taps * capacity].reshape(peers * capacity, taps, -1)
        moved = jnp.take(came, own_box[1:] + after, axis=0)
        new_inner = jnp.concatenate([kept_inner[None], moved[:, :, :own_width]], axis=0)
        new_outer = jnp.concatenate([kept_outer[None], moved[:, :, own_width : own_width + outer_own]], axis=0)
        return placed, out, new_inner, new_outer

    limits = sorted({min(slots - 1, limit) for limit in LIMITS} | {slots - 1})
    pick = sum((needed[0] > limit).astype(jnp.int32) for limit in limits[:-1])
    placed, out, new_inner, new_outer = lax.switch(
        pick, [functools.partial(arrive, limit) for limit in limits],
        got, first_table, near_table, far_table, info, own_box, every, x, xs, window, factors, whole_own, valid_count,
        conv_weight, conv_bias, step_raw[0], skip_row, gate_rows[0], norm_weight[None],
    )
    return (placed.reshape(pool_states.shape), new_inner, new_outer, out[None])


def solution(mesh):
    return jax.shard_map(
        on_device,
        mesh=mesh,
        in_specs=(
            P("req", "seq", None, None), P("req", None, "seq"), P("req", None, "seq"), P("req", None), P("req"),
            P("req", "seq", None), P("req", "seq", None), P("req", "seq", None), P("req", "seq", None), P("req"),
            P(), P(), P(), P(), P(), P(),
        ),
        out_specs=(
            P("req", "seq", None, None), P("req", None, "seq"), P("req", None, "seq"), P("req", "seq", None),
        ),
        check_vma=False,
    )
```

profile of v0, /device:TPU:0, one launch (start us, length us, event | category | flops | bytes accessed | tf_op | source)
XLA Modules:
  0.0 263.9 jit_solution(1424948957897987181)
XLA Ops:
  2.7 2.5 letters.1
  5.2 7.3 %all-to-all-start.3 = ((bf16[8,16,1152]{2,1,0:T(8,128)(2,1)}), bf16[8,16,1152]{2,1,0:T(8,128)(2,1)S(1)}, u32[]{:S(2)}, u32[]{:S(2)}) async-start(bf16[8,16,1152]{2,1,0:T(8,128)(2,1)} %letters.1), calls=%async_computation.3 | async-start | bytes 589824 | tf_op jit(solution)/shard_map/all_to_all | solution.py:578
  16.0 5.5 %pack.1 = bf16[4,13,256,128]{3,2,1,0:T(8,128)(2,1)} custom-call(s32[13]{0:T(128)} %mask_ref.1, f32[13,1024,128]{2,1,0:T(8,128)} %bitcast.214), custom_call_target="tpu_custom_call" | custom-call | flops 34078720 | bytes 10223616 | tf_op jit(solution)/shard_map/pack/pallas_call | solution.py:304
  22.9 4.2 %all-to-all-start.4 = ((bf16[4,13,256,128]{3,2,1,0:T(8,128)(2,1)}), bf16[4,13,256,128]{3,2,1,0:T(8,128)(2,1)S(1)}, u32[]{:S(2)}, u32[]{:S(2)}) async-start(bf16[4,13,256,128]{3,2,1,0:T(8,128)(2,1)} %pack.1), calls=%async_computation.4 | async-start | bytes 6815744 | tf_op jit(solution)/shard_map/all_to_all | solution.py:619
  28.4 1.3 pad_maximum_fusion.18
  29.7 1.3 slice_bitcast_fusion.15
  30.9 1.5 slice_bitcast_fusion.12
  37.9 1.4 multiply_reduce_fusion
  39.9 5.3 %tables.1 = (s32[4,12]{1,0:T(4,128)}, s32[4,12]{1,0:T(4,128)}, s32[1,8]{1,0:T(1,128)}, s32[3,13]{1,0:T(4,128)}, s32[13]{0:T(128)}, /*index=5*/s32[1]{0:T(128)}) custom-call(s32[3]{0:T(128)} %pad_add_fusion.3.place_ref, s32[8,39]{1,0:T(8,128)} %copy-done.22), custom_call_target="tpu_custom_call" | custom-call | flops 1000000 | bytes 4000 | tf_op jit(solution)/shard_map/tables/pallas_call | solution.py:495
  47.2 1.4 dynamic-slice_bitcast_fusion.4
  48.6 1.5 concatenate.110
  50.1 5.7 %all-gather.1 = bf16[4,3,5504]{2,1,0:T(4,128)(2,1)S(1)} all-gather(bf16[1,3,5504]{2,1,0:T(4,128)(2,1)} %bitcast.233), channel_id=2, replica_groups=mesh['req'=8,'seq'=4] {'seq'}, dimensions={0}, use_global_device_ids=true | all-gather | bytes 165120 | tf_op jit(solution)/shard_map/all_gather | solution.py:647
  57.1 1.4 reshape.545
  59.2 1.4 fusion.18
  61.7 1.3 stack.80
  63.8 1.4 fusion.12
  65.6 197.7 %conditional.1 = (bf16[512,4096]{1,0:T(8,128)(2,1)}, f32[13,16,64,128]{3,2,1,0:T(8,128)}, bf16[13,3,1024]{2,0,1:T(8,128)(2,1)S(1)}, bf16[13,3,64]{2,0,1:T(8,128)(2,1)S(1)}) conditional(s32[]{:T(128)} %bitcast.104, (s32[]{:T(128)}, s32[1]{0:T(128)}, s32[]{:T(128)}, bf16[4,13,256,128]{3,2,1,0:T(8,128)(2,1)S(1)}, ...), branch_computations={%region_11.15_spmd, %region_12.16_spmd, %region_13.17_spmd} | conditional | flops 18600208384 | bytes 107894096 | solution.py:738
  65.6 1.3 broadcast_in_dim.213.cb_ref.cbs_ref
  66.9 1.3 broadcast_in_dim.214
  68.3 1.4 broadcast_in_dim_reshape.8.skip_ref
  70.4 2.9 %sort.12 = (bf16[8,256,128]{2,1,0:T(8,128)(2,1)}, s32[1]{0:T(128)}) custom-call(s32[1,8]{1,0:T(1,128)} %get-tuple-element.278.table_ref, bf16[52,256,128]{2,1,0:T(8,128)(2,1)S(1)} %bitcast.202), custom_call_target="tpu_custom_call" | custom-call | flops 2621440 | bytes 1048576 | tf_op jit(solution)/shard_map/cond/branch_1_fun/sort/pallas_call | solution.py:413
  73.3 1.2 broadcast_add_fusion.3.table_ref
  74.5 6.0 %sort.13 = (bf16[9,256,128]{2,1,0:T(8,128)(2,1)}, bf16[9,256,128]{2,1,0:T(8,128)(2,1)}, bf16[9,256,128]{2,1,0:T(8,128)(2,1)}, bf16[9,256,128]{2,1,0:T(8,128)(2,1)}, s32[1]{0:T(128)}) custom-call(s32[4,12]{1,0:T(4,128)} %broadcast_add_fusion.3.table_ref, bf16[52,256,128]{2,1,0:T(8,128)(2,1)S(1)} %bitcast.203), custom_call_target="tpu_custom_call" | custom-call | flops 11796480 | bytes 4718592 | tf_op jit(solution)/shard_map/cond/branch_1_fun/sort/pallas_call | solution.py:413
  80.6 1.3 broadcast_add_fusion.2.table_ref
  81.8 7.3 %sort.14 = (bf16[12,256,128]{2,1,0:T(8,128)(2,1)}, bf16[12,256,128]{2,1,0:T(8,128)(2,1)}, bf16[12,256,128]{2,1,0:T(8,128)(2,1)}, bf16[12,256,128]{2,1,0:T(8,128)(2,1)}, s32[1]{0:T(128)}) custom-call(s32[4,12]{1,0:T(4,128)} %broadcast_add_fusion.2.table_ref, bf16[52,256,128]{2,1,0:T(8,128)(2,1)S(1)} %bitcast.204), custom_call_target="tpu_custom_call" | custom-call | flops 15728640 | bytes 6291456 | tf_op jit(solution)/shard_map/cond/branch_1_fun/sort/pallas_call | solution.py:413
  91.7 25.2 %mix.4 = (bf16[512,4096]{1,0:T(8,128)(2,1)}, bf16[128,4096]{1,0:T(8,128)(2,1)}, f32[512,128]{1,0:T(8,128)}, bf16[512,128]{1,0:T(8,128)(2,1)}) custom-call(s32[1]{0:T(128)S(6)} %add.288.nv_ref, bf16[512,4096]{1,0:T(8,128)(2,1)} %bitcast.236, f32[8,4352]{1,0:T(8,128)} %pad.39.win_ref.wins_ref, f32[4,4352]{1,0:T(4,128)} %get-tuple-element.285.cw_ref.cws_ref, ...), custom_call_target="tpu_custom_call" | custom-call | flops 17179869184 | bytes 8388608 | tf_op jit(solution)/shard_map/cond/branch_1_fun/mix/pallas_call | solution.py:135
  117.0 6.0 %all-to-all-start.1 = ((bf16[8,256,128]{2,1,0:T(8,128)(2,1)}), bf16[8,256,128]{2,1,0:T(8,128)(2,1)S(1)}, u32[]{:S(2)}, u32[]{:S(2)}) async-start(bf16[8,256,128]{2,1,0:T(8,128)(2,1)} %get-tuple-element.298), calls=%async_computation.1 | async-start | bytes 1048576 | tf_op jit(solution)/shard_map/cond/branch_1_fun/all_to_all | solution.py:578
  123.0 2.9 %collective-permute-start.24 = (bf16[9,256,128]{2,1,0:T(8,128)(2,1)}, bf16[9,256,128]{2,1,0:T(8,128)(2,1)}, u32[]{:S(2)}, u32[]{:S(2)}) collective-permute-start(bf16[9,256,128]{2,1,0:T(8,128)(2,1)} %get-tuple-element.310), channel_id=1, source_target_pairs={{0,16},{4,20},{8,24},{12,28},{16,0},{20,4},{24,8},{28,12},{1,17},{... | collective-permute-start | bytes 1769480 | tf_op jit(solution)/shard_map/cond/branch_1_fun/ppermute | solution.py:626
  125.9 1.5 collective-permute-start.25
  127.4 3.3 %collective-permute-start.26 = (bf16[9,256,128]{2,1,0:T(8,128)(2,1)}, bf16[9,256,128]{2,1,0:T(8,128)(2,1)}, u32[]{:S(2)}, u32[]{:S(2)}) collective-permute-start(bf16[9,256,128]{2,1,0:T(8,128)(2,1)} %get-tuple-element.312), channel_id=1, source_target_pairs={{0,24},{4,28},{8,16},{12,20},{16,8},{20,12},{24,0},{28,4},{1,25},{... | collective-permute-start | bytes 1769480 | tf_op jit(solution)/shard_map/cond/branch_1_fun/ppermute | solution.py:626
  136.3 40.6 %all-to-all-done.1 = bf16[8,256,128]{2,1,0:T(8,128)(2,1)S(1)} async-done(((bf16[8,256,128]{2,1,0:T(8,128)(2,1)}), bf16[8,256,128]{2,1,0:T(8,128)(2,1)S(1)}, u32[]{:S(2)}, u32[]{:S(2)}) %all-to-all-start.1) | async-done | bytes 524320 | tf_op jit(solution)/shard_map/cond/branch_1_fun/all_to_all | solution.py:578
  176.9 1.6 collective-permute-start.14
  178.5 2.0 add_convert_fusion.1
  182.4 1.5 gather_fusion.4
  183.9 3.3 %gather_fusion.3 = bf16[3,4096]{1,0:T(4,128)(2,1)S(1)} fusion(bf16[512,4096]{1,0:T(8,128)(2,1)} %bitcast.237, s32[1024]{0:T(1024)S(1)} %pad_clamp_fusion.3), kind=kCustom, calls=%fused_computation.3.clone | custom fusion | bytes 49164 | tf_op jit(solution)/shard_map/cond/branch_1_fun/jit(_take)/gather | solution.py:725
  189.1 1.6 gather_fusion.5
  191.0 1.1 collective-permute-done.19
  192.8 1.2 collective-permute-done.20
  195.0 7.8 %collective-permute-done.17 = bf16[128,2048]{1,0:T(8,128)(2,1)S(1)} collective-permute-done((bf16[128,2048]{1,0:T(8,128)(2,1)}, bf16[128,2048]{1,0:T(8,128)(2,1)S(1)}, u32[]{:S(2)}, u32[]{:S(2)}) %collective-permute-start.17) | collective-permute-done | bytes 524320 | tf_op jit(solution)/shard_map/cond/branch_1_fun/ppermute | solution.py:582
  202.9 3.3 %collective-permute-start.27 = (bf16[9,256,128]{2,1,0:T(8,128)(2,1)}, bf16[9,256,128]{2,1,0:T(8,128)(2,1)}, u32[]{:S(2)}, u32[]{:S(2)}) collective-permute-start(bf16[9,256,128]{2,1,0:T(8,128)(2,1)} %get-tuple-element.313), channel_id=1, source_target_pairs={{0,28},{4,16},{8,20},{12,24},{16,12},{20,0},{24,4},{28,8},{1,29},{... | collective-permute-start | bytes 1769480 | tf_op jit(solution)/shard_map/cond/branch_1_fun/ppermute | solution.py:626
  206.3 1.1 pad_maximum_fusion.7.init_ref
  207.9 2.6 collective-permute-start.23
  210.6 1.0 pad_maximum_fusion.6.refs_1_
  211.6 16.7 %finish.4 = (bf16[512,4096]{1,0:T(8,128)(2,1)}, s32[1]{0:T(128)}) custom-call(s32[2]{0:T(128)} %pad_add_fusion.1.nv_ref, bf16[512,4096]{1,0:T(8,128)(2,1)} %get-tuple-element.292.part_ref, bf16[512,4096]{1,0:T(8,128)(2,1)} %bitcast.209, bf16[512,128]{1,0:T(8,128)(2,1)} %get-tuple-element.294.read_ref, f32[512,128]{1,0:T(8,128)} %get-tuple-element.295.ecum_ref, ...), custom_call_target="tpu_custom_call" | custom-call | flops 1342177280 | bytes 12582912 | tf_op jit(solution)/shard_map/cond/branch_1_fun/finish/pallas_call | solution.py:246
  229.3 10.8 %collective-permute-done.27.refs_7_ = bf16[9,256,128]{2,1,0:T(8,128)(2,1)} collective-permute-done((bf16[9,256,128]{2,1,0:T(8,128)(2,1)}, bf16[9,256,128]{2,1,0:T(8,128)(2,1)}, u32[]{:S(2)}, u32[]{:S(2)}) %collective-permute-start.27) | collective-permute-done | bytes 589856 | tf_op jit(solution)/shard_map/cond/branch_1_fun/ppermute | solution.py:626
  240.1 1.5 collective-permute-done.21.refs_1_
  241.6 16.2 %collective-permute-done.23.refs_3_ = bf16[12,256,128]{2,1,0:T(8,128)(2,1)} collective-permute-done((bf16[12,256,128]{2,1,0:T(8,128)(2,1)}, bf16[12,256,128]{2,1,0:T(8,128)(2,1)}, u32[]{:S(2)}, u32[]{:S(2)}) %collective-permute-start.23) | collective-permute-done | bytes 786464 | tf_op jit(solution)/shard_map/cond/branch_1_fun/ppermute | solution.py:626
  257.8 5.0 %land.4 = f32[13,1024,128]{2,1,0:T(8,128)} custom-call(s32[3,13]{1,0:T(4,128)S(1)} %copy-done.33, f32[128,1024]{1,0:T(8,128)} %convert_add_fusion.4.final_ref, f32[1,1024]{1,0:T(1,128)} %bitcast.247, bf16[1024,128]{1,0:T(8,128)(2,1)} %bitcast.225, bf16[12,256,128]{2,1,0:T(8,128)(2,1)} %get-tuple-element.306.refs_0_, bf16[12,256,128]{2,1,0:T(8,128)(2,1)} %copy-done.14, ...), custom_call_target="tpu_custom_call" | custom-call | flops 34078720 | bytes 10223616 | tf_op jit(solution)/shard_map/cond/branch_1_fun/land/pallas_call | solution.py:559
  (135 shorter events, 29.1 us)
Async XLA Ops:
  5.2 17.1 %all-to-all-start.3 = ((bf16[8,16,1152]{2,1,0:T(8,128)(2,1)}), bf16[8,16,1152]{2,1,0:T(8,128)(2,1)S(1)}, u32[]{:S(2)}, u32[]{:S(2)}) async-start(bf16[8,16,1152]{2,1,0:T(8,128)(2,1)} %letters.1), calls=%async_computation.3 | async-start | bytes 589824 | tf_op jit(solution)/shard_map/all_to_all | solution.py:578
  16.0 5.5 %copy-start.39 = (f32[64]{0:T(128)S(1)}, f32[64]{0:T(128)}, u32[]{:S(2)}) copy-start(f32[64]{0:T(128)} %param.37) | copy-start | bytes 772
  21.7 0.5 copy-start.51
  22.2 43.3 %copy-start.17 = (f32[4096]{0:T(1024)S(1)}, f32[4096]{0:T(1024)}, u32[]{:S(2)}) copy-start(f32[4096]{0:T(1024)} %param.40) | copy-start | bytes 49156
  22.2 0.7 copy-start
  22.9 42.6 %all-to-all-start.4 = ((bf16[4,13,256,128]{3,2,1,0:T(8,128)(2,1)}), bf16[4,13,256,128]{3,2,1,0:T(8,128)(2,1)S(1)}, u32[]{:S(2)}, u32[]{:S(2)}) async-start(bf16[4,13,256,128]{3,2,1,0:T(8,128)(2,1)} %pack.1), calls=%async_computation.4 | async-start | bytes 6815744 | tf_op jit(solution)/shard_map/all_to_all | solution.py:619
  33.4 0.6 copy-start.22
  55.8 0.7 copy-start.16
  70.4 2.9 %copy-start.30 = (s32[4,12]{1,0:T(4,128)S(1)}, s32[4,12]{1,0:T(4,128)}, u32[]{:S(2)}) copy-start(s32[4,12]{1,0:T(4,128)} %get-tuple-element.277) | copy-start | bytes 580 | tf_op jit(solution)/shard_map/cond
  73.3 7.3 %copy-start.27 = (s32[4,12]{1,0:T(4,128)S(1)}, s32[4,12]{1,0:T(4,128)}, u32[]{:S(2)}) copy-start(s32[4,12]{1,0:T(4,128)} %get-tuple-element.276) | copy-start | bytes 580 | tf_op jit(solution)/shard_map/cond
  80.5 9.2 %copy-start.41 = (f32[64]{0:T(128)S(1)}, f32[64]{0:T(128)}, u32[]{:S(2)}) copy-start(f32[64]{0:T(128)} %get-tuple-element.290) | copy-start | bytes 772 | tf_op jit(solution)/shard_map/cond
  80.5 9.2 %copy-start.44 = (f32[64]{0:T(128)S(1)}, f32[64]{0:T(128)}, u32[]{:S(2)}) copy-start(f32[64]{0:T(128)} %get-tuple-element.291) | copy-start | bytes 772 | tf_op jit(solution)/shard_map/cond
  80.6 9.8 %copy-start.11 = (f32[3,4352]{1,0:T(4,128)S(1)}, f32[3,4352]{1,0:T(4,128)}, u32[]{:S(2)}) copy-start(f32[3,4352]{1,0:T(4,128)} %get-tuple-element.284) | copy-start | bytes 156676 | tf_op jit(solution)/shard_map/cond
  91.7 39.0 %copy-start.33 = (s32[3,13]{1,0:T(4,128)S(1)}, s32[3,13]{1,0:T(4,128)}, u32[]{:S(2)}) copy-start(s32[3,13]{1,0:T(4,128)} %get-tuple-element.297.info_ref) | copy-start | bytes 472 | tf_op jit(solution)/shard_map/cond
  91.7 40.8 %copy-start.20 = (f32[6,64]{1,0:T(8,128)S(1)}, f32[6,64]{1,0:T(8,128)}, u32[]{:S(2)}) copy-start(f32[6,64]{1,0:T(8,128)} %get-tuple-element.296) | copy-start | bytes 4612 | tf_op jit(solution)/shard_map/cond
  91.7 41.1 %copy-start.36 = (f32[64]{0:T(128)S(1)}, f32[64]{0:T(128)}, u32[]{:S(2)}) copy-start(f32[64]{0:T(128)} %get-tuple-element.305) | copy-start | bytes 772 | tf_op jit(solution)/shard_map/cond
  116.9 17.8 %copy-start.2 = (bf16[8,16,1152]{2,1,0:T(8,128)(2,1)S(1)}, bf16[8,16,1152]{2,1,0:T(8,128)(2,1)}, u32[]{:S(2)}) copy-start(bf16[8,16,1152]{2,1,0:T(8,128)(2,1)} %get-tuple-element.303) | copy-start | bytes 884740 | tf_op jit(solution)/shard_map/cond
  116.9 61.6 %collective-permute-start.16 = (bf16[128,4096]{1,0:T(8,128)(2,1)}, bf16[128,4096]{1,0:T(8,128)(2,1)S(1)}, u32[]{:S(2)}, u32[]{:S(2)}) collective-permute-start(bf16[128,4096]{1,0:T(8,128)(2,1)} %get-tuple-element.301), channel_id=1, source_target_pairs={{0,1},{1,0},{2,3},{3,2},{4,5},{5,4},{6,7},{7,6},{8,9},{9,8},{10,11... | collective-permute-start | bytes 3145736 | tf_op jit(solution)/shard_map/cond/branch_1_fun/ppermute | solution.py:582
  117.0 59.9 %all-to-all-start.1 = ((bf16[8,256,128]{2,1,0:T(8,128)(2,1)}), bf16[8,256,128]{2,1,0:T(8,128)(2,1)S(1)}, u32[]{:S(2)}, u32[]{:S(2)}) async-start(bf16[8,256,128]{2,1,0:T(8,128)(2,1)} %get-tuple-element.298), calls=%async_computation.1 | async-start | bytes 1048576 | tf_op jit(solution)/shard_map/cond/branch_1_fun/all_to_all | solution.py:578
  123.0 84.5 %collective-permute-start.24 = (bf16[9,256,128]{2,1,0:T(8,128)(2,1)}, bf16[9,256,128]{2,1,0:T(8,128)(2,1)}, u32[]{:S(2)}, u32[]{:S(2)}) collective-permute-start(bf16[9,256,128]{2,1,0:T(8,128)(2,1)} %get-tuple-element.310), channel_id=1, source_target_pairs={{0,16},{4,20},{8,24},{12,28},{16,0},{20,4},{24,8},{28,12},{1,17},{... | collective-permute-start | bytes 1769480 | tf_op jit(solution)/shard_map/cond/branch_1_fun/ppermute | solution.py:626
  125.9 82.0 %collective-permute-start.25 = (bf16[9,256,128]{2,1,0:T(8,128)(2,1)}, bf16[9,256,128]{2,1,0:T(8,128)(2,1)}, u32[]{:S(2)}, u32[]{:S(2)}) collective-permute-start(bf16[9,256,128]{2,1,0:T(8,128)(2,1)} %get-tuple-element.311), channel_id=1, source_target_pairs={{0,20},{4,24},{8,28},{12,16},{16,4},{20,8},{24,12},{28,0},{1,21},{... | collective-permute-start | bytes 1769480 | tf_op jit(solution)/shard_map/cond/branch_1_fun/ppermute | solution.py:626
  127.4 101.9 %collective-permute-start.26 = (bf16[9,256,128]{2,1,0:T(8,128)(2,1)}, bf16[9,256,128]{2,1,0:T(8,128)(2,1)}, u32[]{:S(2)}, u32[]{:S(2)}) collective-permute-start(bf16[9,256,128]{2,1,0:T(8,128)(2,1)} %get-tuple-element.312), channel_id=1, source_target_pairs={{0,24},{4,28},{8,16},{12,20},{16,8},{20,12},{24,0},{28,4},{1,25},{... | collective-permute-start | bytes 1769480 | tf_op jit(solution)/shard_map/cond/branch_1_fun/ppermute | solution.py:626
  132.7 0.6 copy-start.24
  135.6 51.9 %copy-start.47 = (s32[13]{0:T(128)S(1)}, s32[13]{0:T(128)}, u32[]{:S(2)}) copy-start(s32[13]{0:T(128)} %get-tuple-element.304) | copy-start | bytes 160 | tf_op jit(solution)/shard_map/cond
  176.9 29.4 %copy-start.8 = (bf16[4,256,128]{2,1,0:T(8,128)(2,1)}, bf16[4,256,128]{2,1,0:T(8,128)(2,1)S(1)}, u32[]{:S(2)}) copy-start(bf16[4,256,128]{2,1,0:T(8,128)(2,1)S(1)} %dynamic-slice_select_fusion.1) | copy-start | bytes 786436 | tf_op jit(solution)/shard_map/cond
  176.9 15.8 %collective-permute-start.14 = (bf16[1,1024,128]{2,1,0:T(8,128)(2,1)S(1)}, bf16[1,1024,128]{2,1,0:T(8,128)(2,1)S(1)}, u32[]{:S(2)}, u32[]{:S(2)}) collective-permute-start(bf16[1,1024,128]{2,1,0:T(8,128)(2,1)S(1)} %bitcast.222), channel_id=1, source_target_pairs={{0,2},{1,3},{2,0},{3,1},{4,6},{5,7},{6,4},{7,5},{8,10},{9,11},{10,... | collective-permute-start | bytes 786440 | tf_op jit(solution)/shard_map/cond/branch_1_fun/ppermute | solution.py:582
  178.5 10.7 %copy-start.5 = (bf16[128,4096]{1,0:T(8,128)(2,1)}, bf16[128,4096]{1,0:T(8,128)(2,1)S(1)}, u32[]{:S(2)}) copy-start(bf16[128,4096]{1,0:T(8,128)(2,1)S(1)} %collective-permute-done.16.refs_0_) | copy-start | bytes 3145732 | tf_op jit(solution)/shard_map/cond
  182.4 8.5 %copy-start.50 = (pred[3]{0:T(512)(128)(4,1)}, pred[3]{0:T(512)(128)(4,1)S(1)}, u32[]{:S(2)}) copy-start(pred[3]{0:T(512)(128)(4,1)S(1)} %compare_and_fusion.5) | copy-start | bytes 13 | tf_op jit(solution)/shard_map/cond
  187.7 4.4 %collective-permute-start.19 = (bf16[1,3,4352]{2,1,0:T(4,128)(2,1)S(1)}, bf16[1,3,4352]{2,1,0:T(4,128)(2,1)S(1)}, u32[]{:S(2)}, u32[]{:S(2)}) collective-permute-start(bf16[1,3,4352]{2,1,0:T(4,128)(2,1)S(1)} %maximum_select_fusion.3), channel_id=1, source_target_pairs={{0,2},{1,3},{2,0},{3,1},{4,6},{5,7},{6,4},{7,5},{8,10},{9,11},{10,... | collective-permute-start | bytes 78344 | tf_op jit(solution)/shard_map/cond/branch_1_fun/ppermute | solution.py:582
  192.1 10.7 %collective-permute-start.17 = (bf16[128,2048]{1,0:T(8,128)(2,1)}, bf16[128,2048]{1,0:T(8,128)(2,1)S(1)}, u32[]{:S(2)}, u32[]{:S(2)}) collective-permute-start(bf16[128,2048]{1,0:T(8,128)(2,1)} %constant_dynamic-slice_fusion.3), channel_id=1, source_target_pairs={{0,2},{1,3},{2,0},{3,1},{4,6},{5,7},{6,4},{7,5},{8,10},{9,11},{10,... | collective-permute-start | bytes 1572872 | tf_op jit(solution)/shard_map/cond/branch_1_fun/ppermute | solution.py:582
  192.7 1.3 collective-permute-start.20
  194.0 8.9 %collective-permute-start.15 = (bf16[2,1024,128]{2,1,0:T(8,128)(2,1)S(1)}, bf16[2,1024,128]{2,1,0:T(8,128)(2,1)S(1)}, u32[]{:S(2)}, u32[]{:S(2)}) collective-permute-start(bf16[2,1024,128]{2,1,0:T(8,128)(2,1)S(1)} %pad_maximum_fusion.8), channel_id=1, source_target_pairs={{0,1},{1,0},{2,3},{3,2},{4,5},{5,4},{6,7},{7,6},{8,9},{9,8},{10,11... | collective-permute-start | bytes 1572872 | tf_op jit(solution)/shard_map/cond/branch_1_fun/ppermute | solution.py:582
  202.8 4.6 %collective-permute-start.18 = (bf16[128,2048]{1,0:T(8,128)(2,1)S(1)}, bf16[128,2048]{1,0:T(8,128)(2,1)S(1)}, u32[]{:S(2)}, u32[]{:S(2)}) collective-permute-start(bf16[128,2048]{1,0:T(8,128)(2,1)S(1)} %collective-permute-done.17), channel_id=1, source_target_pairs={{0,1},{1,0},{2,3},{3,2},{4,5},{5,4},{6,7},{7,6},{8,9},{9,8},{10,11... | collective-permute-start | bytes 1572872 | tf_op jit(solution)/shard_map/cond/branch_1_fun/ppermute | solution.py:582
  202.9 37.2 %collective-permute-start.27 = (bf16[9,256,128]{2,1,0:T(8,128)(2,1)}, bf16[9,256,128]{2,1,0:T(8,128)(2,1)}, u32[]{:S(2)}, u32[]{:S(2)}) collective-permute-start(bf16[9,256,128]{2,1,0:T(8,128)(2,1)} %get-tuple-element.313), channel_id=1, source_target_pairs={{0,28},{4,16},{8,20},{12,24},{16,12},{20,0},{24,4},{28,8},{1,29},{... | collective-permute-start | bytes 1769480 | tf_op jit(solution)/shard_map/cond/branch_1_fun/ppermute | solution.py:626
  207.4 34.2 %collective-permute-start.21 = (bf16[12,256,128]{2,1,0:T(8,128)(2,1)}, bf16[12,256,128]{2,1,0:T(8,128)(2,1)S(1)}, u32[]{:S(2)}, u32[]{:S(2)}) collective-permute-start(bf16[12,256,128]{2,1,0:T(8,128)(2,1)} %get-tuple-element.307), channel_id=1, source_target_pairs={{0,4},{4,8},{8,12},{12,0},{16,20},{20,24},{24,28},{28,16},{1,5},{5... | collective-permute-start | bytes 2359304 | tf_op jit(solution)/shard_map/cond/branch_1_fun/ppermute | solution.py:626
  207.5 34.1 %collective-permute-start.22 = (bf16[12,256,128]{2,1,0:T(8,128)(2,1)}, bf16[12,256,128]{2,1,0:T(8,128)(2,1)}, u32[]{:S(2)}, u32[]{:S(2)}) collective-permute-start(bf16[12,256,128]{2,1,0:T(8,128)(2,1)} %get-tuple-element.308), channel_id=1, source_target_pairs={{0,8},{4,12},{8,0},{12,4},{16,24},{20,28},{24,16},{28,20},{1,9},{5... | collective-permute-start | bytes 2359304 | tf_op jit(solution)/shard_map/cond/branch_1_fun/ppermute | solution.py:626
  207.9 49.8 %collective-permute-start.23 = (bf16[12,256,128]{2,1,0:T(8,128)(2,1)}, bf16[12,256,128]{2,1,0:T(8,128)(2,1)}, u32[]{:S(2)}, u32[]{:S(2)}) collective-permute-start(bf16[12,256,128]{2,1,0:T(8,128)(2,1)} %get-tuple-element.309), channel_id=1, source_target_pairs={{0,12},{4,0},{8,4},{12,8},{16,28},{20,16},{24,20},{28,24},{1,13},{... | collective-permute-start | bytes 2359304 | tf_op jit(solution)/shard_map/cond/branch_1_fun/ppermute | solution.py:626
  211.6 16.7 %dynamic-slice-start.1 = ((f32[4096]{0:T(1024)}, s32[]{:T(128)}), f32[1024]{0:T(1024)S(1)}, s32[]{:S(2)}) async-start(f32[4096]{0:T(1024)} %copy-done.24, s32[]{:T(128)} %select_n.363), calls=%async_computation.6 | async-start | bytes 8704 | tf_op jit(solution)/shard_map/dynamic-slice.6
  241.6 16.2 %copy-start.14 = (bf16[12,256,128]{2,1,0:T(8,128)(2,1)}, bf16[12,256,128]{2,1,0:T(8,128)(2,1)S(1)}, u32[]{:S(2)}) copy-start(bf16[12,256,128]{2,1,0:T(8,128)(2,1)S(1)} %collective-permute-done.21.refs_1_) | copy-start | bytes 2359300 | tf_op jit(solution)/shard_map/cond
  263.2 0.6 copy-start.18
  263.2 0.6 copy-start.38
where the time goes:
time: 266 us; the launch traced here: 264 us
  waiting for transfers between devices  79.5 us (30%)
  Pallas kernels  76.2 us (29%)
  starting transfers between devices  34.5 us (13%)
  local copies, waits for them, and re-layouts  33.3 us (13%)
  other arithmetic  24.6 us (9%)
  blocking collectives  5.74 us (2%)
  between operations  5.36 us (2%)
  loops' own time  4.73 us (2%)
    all_to_all x2, waiting for transfers between devices, exchange(): lax.all_to_all(source, 'req', split_axis=0, concat_axis=0, tiled=True)  40.6 us
    ppermute x7, waiting for transfers between devices, hop(): return lax.ppermute(value, 'req', pairs)  28.5 us
    pallas_call x1, Pallas kernels, mix(): pl.pallas_call(mix_kernel, grid_spec=pltpu.PrefetchScalarGridSpec(num_sca...  25.2 us
    pallas_call x1, Pallas kernels, finish(): pl.pallas_call(finish_kernel, grid_spec=pltpu.PrefetchScalarGridSpec(num_...  16.7 us
    pallas_call x3, Pallas kernels, sort_pieces(): pl.pallas_call(sort_kernel, in_specs=[smem, whole], out_specs=[whole] * p...  16.1 us
    ppermute x7, starting transfers between devices, hop(): return lax.ppermute(value, 'req', pairs)  14 us
    all_to_all x2, starting transfers between devices, exchange(): lax.all_to_all(source, 'req', split_axis=0, concat_axis=0, tiled=True)  13.3 us
    ppermute x7, waiting for transfers between devices, flip(): lax.ppermute(value, axis, [(r, r ^ step) for r in range(lax.axis_size(axi...  10.1 us
  transfers between devices with their start and end apart: 17, of which 8 were waited for; matrix products, arithmetic and copies ran while one was open for 17% of the time, Pallas kernels for 10%

commit v1 on v0

--- a/solution.py
+++ b/solution.py
@@ -386,44 +386,51 @@
     )(plan.T, mask, jnp.moveaxis(inner_window, 1, 0), jnp.moveaxis(outer_window, 1, 0), plan_row)
 
 
-def sort_kernel(table_ref, got_ref, *refs):
-    stage, in_sem, out_sem = refs[-3:]
-    outs, token_ref = refs[:-4], refs[-4]
-    parts, count = stage.shape[:2]
-    token_ref[0] = 0
-
-    def one(k, carry):
+def sort_kernel(sizes, turn_ref, *refs):
+    tables, got_ref = refs[: len(sizes)], refs[len(sizes)]
+    refs = refs[len(sizes) + 1 :]
+    total = sum(parts for parts, _ in sizes)
+    outs, token_ref = refs[:total], refs[total]
+    stages, in_sem, out_sem = refs[total + 1 : total + 1 + len(sizes)], refs[-2], refs[-1]
+    token_ref[0] = turn_ref[0]
+    number = 0
+    for (parts, count), table_ref, stage in zip(sizes, tables, stages):
+
+        def one(k, carry, parts=parts, table_ref=table_ref, stage=stage, number=number):
+            for m in range(parts):
+                pltpu.make_async_copy(got_ref.at[table_ref[m, k]], stage.at[m, k], in_sem.at[number + m]).start()
+            return carry
+
+        lax.fori_loop(0, count, one, 0)
+        number += parts
+    copies = []
+    for (parts, count), stage in zip(sizes, stages):
         for m in range(parts):
-            pltpu.make_async_copy(got_ref.at[table_ref[m, k]], stage.at[m, k], in_sem.at[m]).start()
-        return carry
-
-    lax.fori_loop(0, count, one, 0)
-    copies = [pltpu.make_async_copy(stage.at[m], outs[m], out_sem.at[m]) for m in range(parts)]
-    for m in range(parts):
-        pltpu.make_async_copy(got_ref.at[0:count], stage.at[m], in_sem.at[m]).wait()
-        copies[m].start()
+            pltpu.make_async_copy(got_ref.at[0:count], stage.at[m], in_sem.at[len(copies)]).wait()
+            copies.append(pltpu.make_async_copy(stage.at[m], outs[len(copies)], out_sem.at[len(copies)]))
+            copies[-1].start()
     for copy in copies:
         copy.wait()
 
 
-def sort_pieces(table, got, count):
-    parts = table.shape[0]
+def sort_pieces(turn, got, *jobs):
     rows, lanes = got.shape[1:]
+    sizes = [(table.shape[0], count) for table, count in jobs]
+    total = sum(parts for parts, _ in sizes)
     smem, whole = pl.BlockSpec(memory_space=pltpu.SMEM), pl.BlockSpec(memory_space=pl.ANY)
-    *outs, token = pl.pallas_call(
-        sort_kernel,
-        in_specs=[smem, whole],
-        out_specs=[whole] * parts + [smem],
-        out_shape=[jax.ShapeDtypeStruct((count, rows, lanes), jnp.bfloat16)] * parts + [jax.ShapeDtypeStruct((1,), jnp.int32)],
-        scratch_shapes=[
-            pltpu.VMEM((parts, count, rows, lanes), jnp.bfloat16),
-            pltpu.SemaphoreType.DMA((parts,)),
-            pltpu.SemaphoreType.DMA((parts,)),
-        ],
-        cost_estimate=pl.CostEstimate(flops=10 * parts * count * rows * lanes, bytes_accessed=4 * parts * count * rows * lanes, transcendentals=0),
+    work = sum(parts * count for parts, count in sizes) * rows * lanes
+    outs = pl.pallas_call(
+        functools.partial(sort_kernel, sizes),
+        in_specs=[smem] * (1 + len(jobs)) + [whole],
+        out_specs=[whole] * total + [smem],
+        out_shape=[jax.ShapeDtypeStruct((count, rows, lanes), jnp.bfloat16) for parts, count in sizes for _ in range(parts)]
+        + [jax.ShapeDtypeStruct((1,), jnp.int32)],
+        scratch_shapes=[pltpu.VMEM((parts, count, rows, lanes), jnp.bfloat16) for parts, count in sizes]
+        + [pltpu.SemaphoreType.DMA((total,)), pltpu.SemaphoreType.DMA((total,))],
+        cost_estimate=pl.CostEstimate(flops=10 * work, bytes_accessed=4 * work, transcendentals=0),
         name="sort",
-    )(table, got)
-    return outs, token[0]
+    )(turn, *[table for table, _ in jobs], got)
+    return outs[:-1], outs[-1]
 
 
 def tables_kernel(peers, parts, slots, capacity, place_ref, plan_ref, near_ref, far_ref, first_ref, info_ref, box_ref, need_ref, inverse):
@@ -466,25 +473,28 @@
 
             @pl.when(d == me)
             def _():
-                info_ref[0, k] = jnp.where(live, jnp.where(far, 2, 1), 0)
-                info_ref[1, k] = count
-                info_ref[2, k] = seat
-
-            @pl.when(k == 0)
+                info_ref[0, k] = jnp.where(live, jnp.where(far, jnp.where(count == 0, 3, 2), 1), 0)
+                info_ref[1, k] = count - 1
+                info_ref[2, k] = jnp.where(k == 0, 0, jnp.where(k == 1, seat, (1 - side) * parts))
+
+            here = live & (r_side == side)
+
+            @pl.when(here & ((far & (count == 0)) | ((k == 0) & ~far)))
             def _():
-                first_ref[0, d] = jnp.where(live & (r_side == side), held, 0)
-
-            @pl.when(live & (k > 0) & (r_side == side) & (d_side == side))
+                first_ref[0, d] = held
+
+            @pl.when(here & (k > 0) & ~far)
             def _():
                 near_ref[m, k - 1] = held
 
-            @pl.when(far & (k > 0) & (r_side == side))
+            @pl.when(here & far & (count > 0))
             def _():
-                far_ref[m, count] = held
-
-            return count + (far & (k > 0)).astype(jnp.int32)
-
-        return jnp.maximum(most, lax.fori_loop(0, slots, one_slot, 0))
+                far_ref[m, count - 1] = held
+
+            return count + far.astype(jnp.int32)
+
+        first_ref[0, d] = 0
+        return jnp.maximum(most, lax.fori_loop(0, slots, one_slot, 0) - 1)
 
     need_ref[0] = lax.fori_loop(0, peers, one_target, 0)
 
@@ -503,7 +513,7 @@
     )(place, plan)
 
 
-def land_kernel(parts, info_ref, final_ref, whole_ref, initial_ref, *refs):
+def land_kernel(parts, info_ref, final_ref, whole_ref, initial_ref, first_ref, *refs):
     near, far = refs[:parts], refs[parts : 2 * parts]
     out_ref, held, wide, in_sem, out_sem = refs[2 * parts :]
     rest, rows, _ = near[0].shape
@@ -511,15 +521,22 @@
 
     def each(k, act):
         kind, at = info_ref[0, k], info_ref[1, k]
-        for m in range(parts):
-
-            @pl.when(kind == 1)
-            def _():
+
+        @pl.when(kind == 1)
+        def _():
+            for m in range(parts):
                 act(pltpu.make_async_copy(near[m].at[k - 1], held.at[k, m], in_sem.at[k]))
 
-            @pl.when(kind == 2)
-            def _():
+        @pl.when(kind == 2)
+        def _():
+            for m in range(parts):
                 act(pltpu.make_async_copy(far[m].at[at], held.at[k, m], in_sem.at[k]))
+
+        @pl.when(kind == 3)
+        def _():
+            for m in range(parts):
+                sender = info_ref[2, 2] + lax.rem(info_ref[2, 1] + parts - m, parts)
+                act(pltpu.make_async_copy(first_ref.at[sender], held.at[k, m], in_sem.at[k]))
 
     def store(k):
         return pltpu.make_async_copy(wide.at[k], out_ref.at[k], out_sem.at[k])
@@ -551,14 +568,14 @@
     lax.fori_loop(0, slots, third, 0)
 
 
-def land(info, final, whole_own, initial_own, near, far):
+def land(info, final, whole_own, initial_own, first, near, far):
     parts = len(near)
     rest, rows, lanes = near[0].shape
     slots = rest + 1
     smem, vmem, whole = (pl.BlockSpec(memory_space=space) for space in (pltpu.SMEM, pltpu.VMEM, pl.ANY))
     return pl.pallas_call(
         functools.partial(land_kernel, parts),
-        in_specs=[smem, vmem, vmem, vmem] + [whole] * (2 * parts),
+        in_specs=[smem, vmem, vmem, vmem] + [whole] * (2 * parts + 1),
         out_specs=whole,
         out_shape=jax.ShapeDtypeStruct((slots, parts * rows, lanes), jnp.float32),
         scratch_shapes=[
@@ -571,7 +588,7 @@
             flops=20 * slots * parts * rows * lanes, bytes_accessed=6 * slots * parts * rows * lanes, transcendentals=0
         ),
         name="land",
-    )(info, final, whole_own, initial_own, *near, *far)
+    )(info, final, whole_own, initial_own, first, *near, *far)
 
 
 def exchange(source):
@@ -592,7 +609,7 @@
     return [held[m] for m in sorted(held)]
 
 
-LIMITS = (7, 9)
+LIMITS = (8, 10)
 
 
 def on_device(
@@ -679,14 +696,13 @@
         limit, got, first_table, near_table, far_table, info, own_box, every, x, xs, window, factors, whole_own, valid_count,
         conv_weight, conv_bias, step_raw, skip_row, gate, norm,
     ):
-        first, token = sort_pieces(first_table, got, peers)
-        first = exchange(first[0])
-        far_all, token = sort_pieces(far_table + token, got, limit)
-        far = [hop(far_all[m], 1, m) for m in range(parts)]
-        near_all, token = sort_pieces(near_table + token, got, slots - 1)
+        sorted_pieces, token = sort_pieces(jnp.zeros((1,), jnp.int32), got, (first_table, peers), (far_table, limit))
+        first = exchange(sorted_pieces[0])
+        far = [hop(sorted_pieces[1 + m], 1, m) for m in range(parts)]
+        near_all, token = sort_pieces(token, got, (near_table, slots - 1))
         near = [near_all[0]] + [hop(near_all[m], 0, m) for m in range(1, parts)]
         part, end, ecum, read = mix(
-            valid_count + token, x, xs, window, conv_weight, conv_bias, step_raw, step_bias, decay_log, skip_row
+            valid_count + token[0], x, xs, window, conv_weight, conv_bias, step_raw, step_bias, decay_log, skip_row
         )
         ends, total = [], end
         step = 1
@@ -718,7 +734,7 @@
         out, token = finish(
             jnp.concatenate([valid_count, rank[None]]), part, gate, read, ecum, ends, factors, initial, norm
         )
-        placed = land(info, final, whole_own, initial_own, near, far)
+        placed = land(info, final, whole_own, initial_own, first, near, far)
         position = lengths[0] + after - taps + jnp.arange(taps, dtype=jnp.int32) - rank * length
         inside = (position >= 0) & (position < length)
         clipped = jnp.clip(position, 0, length - 1)

time: 266 us -> 250 us (0.940)
  waiting for transfers between devices: 79.5 us -> 73.2 us
  local copies, waits for them, and re-layouts: 33.3 us -> 28.5 us
    all_to_all x2, waiting for transfers between devices: 40.6 us -> 5.28 us  [exchange(): lax.all_to_all(source, 'req', split_axis=0, concat_axis=0, tiled=True)]
    ppermute x7, waiting for transfers between devices: 28.5 us -> 53.6 us  [hop(): return lax.ppermute(value, 'req', pairs)]
    all_to_all x1, waiting for transfers between devices: 0.35 us -> 5.99 us  [on_device(): lax.all_to_all(packed, 'req', 0, 0, axis_index_groups=groups, tiled=True)]
    pallas_call x3 -> x2, Pallas kernels: 16.1 us -> 14.2 us  [sort_pieces(): pl.pallas_call(functools.partial(sort_kernel, sizes), in_specs=[smem] * (...]
  transfers between devices with their start and end apart: 17 -> 17, of which waited for: 8 -> 8; matrix products, arithmetic and copies ran while one was open for 17% -> 18% of each run, Pallas kernels for 10% -> 11%
where the time goes in v1:
time: 250 us; the launch traced here: 248 us
  Pallas kernels  74.7 us (30%)
  waiting for transfers between devices  73.2 us (29%)
  starting transfers between devices  32 us (13%)
  local copies, waits for them, and re-layouts  28.5 us (11%)
  other arithmetic  24.3 us (10%)
  blocking collectives  5.74 us (2%)
  between operations  5.53 us (2%)
  loops' own time  4.48 us (2%)
    ppermute x7, waiting for transfers between devices, hop(): return lax.ppermute(value, 'req', pairs)  53.6 us
    pallas_call x1, Pallas kernels, mix(): pl.pallas_call(mix_kernel, grid_spec=pltpu.PrefetchScalarGridSpec(num_sca...  25.2 us
    pallas_call x1, Pallas kernels, finish(): pl.pallas_call(finish_kernel, grid_spec=pltpu.PrefetchScalarGridSpec(num_...  16.7 us
    pallas_call x2, Pallas kernels, sort_pieces(): pl.pallas_call(functools.partial(sort_kernel, sizes), in_specs=[smem] * (...  14.2 us
    ppermute x7, starting transfers between devices, hop(): return lax.ppermute(value, 'req', pairs)  12.1 us
    all_to_all x2, starting transfers between devices, exchange(): lax.all_to_all(source, 'req', split_axis=0, concat_axis=0, tiled=True)  12.1 us
    ppermute x7, waiting for transfers between devices, flip(): lax.ppermute(value, axis, [(r, r ^ step) for r in range(lax.axis_size(axi...  8.29 us
    all_to_all x1, waiting for transfers between devices, on_device(): lax.all_to_all(packed, 'req', 0, 0, axis_index_groups=groups, tiled=True)  5.99 us
  transfers between devices with their start and end apart: 17, of which 8 were waited for; matrix products, arithmetic and copies ran while one was open for 18% of the time, Pallas kernels for 11%

profile of v1, /device:TPU:0, one launch (start us, length us, event | category | flops | bytes accessed | tf_op | source)
XLA Modules:
  0.0 248.5 jit_solution(15710076778637114223)
XLA Ops:
  2.7 2.5 letters.1
  5.2 7.3 %all-to-all-start.3 = ((bf16[8,16,1152]{2,1,0:T(8,128)(2,1)}), bf16[8,16,1152]{2,1,0:T(8,128)(2,1)S(1)}, u32[]{:S(2)}, u32[]{:S(2)}) async-start(bf16[8,16,1152]{2,1,0:T(8,128)(2,1)} %letters.1), calls=%async_computation.3 | async-start | bytes 589824 | tf_op jit(solution)/shard_map/all_to_all | solution.py:595
  15.0 1.0 copy.46
  16.0 5.5 %pack.1 = bf16[4,13,256,128]{3,2,1,0:T(8,128)(2,1)} custom-call(s32[13]{0:T(128)} %mask_ref.1, f32[13,1024,128]{2,1,0:T(8,128)} %bitcast.205), custom_call_target="tpu_custom_call" | custom-call | flops 34078720 | bytes 10223616 | tf_op jit(solution)/shard_map/pack/pallas_call | solution.py:304
  22.8 3.9 %all-to-all-start.4 = ((bf16[4,13,256,128]{3,2,1,0:T(8,128)(2,1)}), bf16[4,13,256,128]{3,2,1,0:T(8,128)(2,1)S(1)}, u32[]{:S(2)}, u32[]{:S(2)}) async-start(bf16[4,13,256,128]{3,2,1,0:T(8,128)(2,1)} %pack.1), calls=%async_computation.4 | async-start | bytes 6815744 | tf_op jit(solution)/shard_map/all_to_all | solution.py:636
  27.8 1.3 slice_bitcast_fusion.15
  29.1 1.5 slice_bitcast_fusion.12
  30.6 1.0 copy.45
  36.6 0.8 dynamic-slice_bitcast_fusion.4
  37.4 1.5 concatenate.110
  38.9 5.7 %all-gather.1 = bf16[4,3,5504]{2,1,0:T(4,128)(2,1)S(1)} all-gather(bf16[1,3,5504]{2,1,0:T(4,128)(2,1)} %bitcast.224), channel_id=2, replica_groups=mesh['req'=8,'seq'=4] {'seq'}, dimensions={0}, use_global_device_ids=true | all-gather | bytes 165120 | tf_op jit(solution)/shard_map/all_gather | solution.py:664
  46.0 5.7 %tables.1 = (s32[4,12]{1,0:T(4,128)S(1)}, s32[4,12]{1,0:T(4,128)S(1)}, s32[1,8]{1,0:T(1,128)}, s32[3,13]{1,0:T(4,128)}, s32[13]{0:T(128)}, /*index=5*/s32[1]{0:T(128)}) custom-call(s32[3]{0:T(128)} %pad_add_fusion.3.place_ref, s32[8,39]{1,0:T(8,128)} %copy-done.32), custom_call_target="tpu_custom_call" | custom-call | flops 1000000 | bytes 4000 | tf_op jit(solution)/shard_map/tables/pallas_call | solution.py:505
  52.9 0.8 convert_reduce_fusion
  53.7 1.4 fusion.18
  56.9 0.8 dynamic-slice_bitcast_fusion.3
  57.7 1.4 fusion.12
  59.1 6.0 %all-to-all-done.4 = bf16[4,13,256,128]{3,2,1,0:T(8,128)(2,1)S(1)} async-done(((bf16[4,13,256,128]{3,2,1,0:T(8,128)(2,1)}), bf16[4,13,256,128]{3,2,1,0:T(8,128)(2,1)S(1)}, u32[]{:S(2)}, u32[]{:S(2)}) %all-to-all-start.4) | async-done | bytes 3407904 | tf_op jit(solution)/shard_map/all_to_all | solution.py:636
  65.1 183.2 %conditional.1 = (bf16[512,4096]{1,0:T(8,128)(2,1)}, f32[13,16,64,128]{3,2,1,0:T(8,128)}, bf16[13,3,1024]{2,0,1:T(8,128)(2,1)}, bf16[13,3,64]{2,0,1:T(8,128)(2,1)}) conditional(s32[]{:T(128)} %bitcast.98, (s32[]{:T(128)}, s32[1]{0:T(128)}, s32[]{:T(128)}, bf16[4,13,256,128]{3,2,1,0:T(8,128)(2,1)S(1)}, s32[1,8]{1,0:T(1,128)}, ...), branch_computations={%region_11.15_spmd, %region_12.16_spmd, %region_13.17_spmd} | conditional | flops 18600208384 | bytes 120533168 | solution.py:754
  67.2 1.3 broadcast_in_dim.196.cb_ref.cbs_ref
  68.6 6.4 %sort.6 = (bf16[8,256,128]{2,1,0:T(8,128)(2,1)}, bf16[8,256,128]{2,1,0:T(8,128)(2,1)}, bf16[8,256,128]{2,1,0:T(8,128)(2,1)}, bf16[8,256,128]{2,1,0:T(8,128)(2,1)...) custom-call(s32[1]{0:T(128)} %constant.317.clone.turn_ref, s32[1,8]{1,0:T(1,128)} %get-tuple-element.235.refs_0_, ...), custom_call_target="tpu_custom_call" | custom-call | flops 13107200 | bytes 5242880 | tf_op jit(solution)/shard_map/cond/branch_0_fun/sort/pallas_call | solution.py:422
  75.0 7.8 %sort.7 = (bf16[12,256,128]{2,1,0:T(8,128)(2,1)}, bf16[12,256,128]{2,1,0:T(8,128)(2,1)}, bf16[12,256,128]{2,1,0:T(8,128)(2,1)}, bf16[12,256,128]{2,1,0:T(8,128)(2,1)}, s32[1]{0:T(128)}) custom-call(s32[1]{0:T(128)} %get-tuple-element.238.turn_ref, s32[4,12]{1,0:T(4,128)S(1)} %get-tuple-element.239.refs_0_, bf16[52,256,128]{2,1,0:T(8,128)(2,1)S(1)} %bitcast.194), custom_call_target="tpu_custom_call" | custom-call | flops 15728640 | bytes 6291456 | tf_op jit(solution)/shard_map/cond/branch_0_fun/sort/pallas_call | solution.py:422
  85.4 25.2 %mix.3 = (bf16[512,4096]{1,0:T(8,128)(2,1)}, bf16[128,4096]{1,0:T(8,128)(2,1)}, f32[512,128]{1,0:T(8,128)}, bf16[512,128]{1,0:T(8,128)(2,1)}) custom-call(s32[1]{0:T(128)S(6)} %add.228.nv_ref, bf16[512,4096]{1,0:T(8,128)(2,1)} %bitcast.225, f32[8,4352]{1,0:T(8,128)} %pad.34.win_ref.wins_ref, f32[4,4352]{1,0:T(4,128)} %get-tuple-element.243.cw_ref.cws_ref, ...), custom_call_target="tpu_custom_call" | custom-call | flops 17179869184 | bytes 8388608 | tf_op jit(solution)/shard_map/cond/branch_0_fun/mix/pallas_call | solution.py:135
  110.7 4.8 %all-to-all-start = ((bf16[8,256,128]{2,1,0:T(8,128)(2,1)}), bf16[8,256,128]{2,1,0:T(8,128)(2,1)S(1)}, u32[]{:S(2)}, u32[]{:S(2)}) async-start(bf16[8,256,128]{2,1,0:T(8,128)(2,1)} %get-tuple-element.256), calls=%async_computation | async-start | bytes 1048576 | tf_op jit(solution)/shard_map/cond/branch_0_fun/all_to_all | solution.py:595
  115.5 2.0 collective-permute-start.7
  117.5 1.5 collective-permute-start.8
  119.0 2.4 collective-permute-start.10
  122.6 1.2 slice.124
  126.6 4.9 %all-to-all-done.first_ref = bf16[8,256,128]{2,1,0:T(8,128)(2,1)S(1)} async-done(((bf16[8,256,128]{2,1,0:T(8,128)(2,1)}), bf16[8,256,128]{2,1,0:T(8,128)(2,1)S(1)}, u32[]{:S(2)}, u32[]{:S(2)}) %all-to-all-start) | async-done | bytes 524320 | tf_op jit(solution)/shard_map/cond/branch_0_fun/all_to_all | solution.py:595
  131.6 1.6 collective-permute-start
  133.2 2.0 add_convert_fusion
  137.1 3.3 %gather_fusion = bf16[3,4096]{1,0:T(4,128)(2,1)S(1)} fusion(bf16[512,4096]{1,0:T(8,128)(2,1)} %bitcast.226, s32[1024]{0:T(1024)S(1)} %pad_clamp_fusion.1), kind=kCustom, calls=%fused_computation.clone | custom fusion | bytes 49164 | tf_op jit(solution)/shard_map/cond/branch_0_fun/jit(_take)/gather | solution.py:741
  140.5 1.5 gather_fusion.1
  146.2 0.8 broadcast_select_fusion.2
  147.9 1.5 collective-permute-start.3
  149.4 0.8 pad_maximum_fusion.4
  150.4 1.2 collective-permute-done.6
  151.7 0.9 fusion.1
  152.7 7.0 %collective-permute-done.3 = bf16[128,2048]{1,0:T(8,128)(2,1)S(1)} collective-permute-done((bf16[128,2048]{1,0:T(8,128)(2,1)S(1)}, bf16[128,2048]{1,0:T(8,128)(2,1)S(1)}, u32[]{:S(2)}, u32[]{:S(2)}) %collective-permute-start.3) | collective-permute-done | bytes 524320 | tf_op jit(solution)/shard_map/cond/branch_0_fun/ppermute | solution.py:599
  161.5 1.1 pad_maximum_fusion.1.init_ref
  162.6 1.8 collective-permute-start.9
  164.5 1.3 collective-permute-start.12
  165.7 21.2 %collective-permute-done.11.refs_5_ = bf16[8,256,128]{2,1,0:T(8,128)(2,1)} collective-permute-done((bf16[8,256,128]{2,1,0:T(8,128)(2,1)S(1)}, bf16[8,256,128]{2,1,0:T(8,128)(2,1)}, u32[]{:S(2)}, u32[]{:S(2)}) %collective-permute-start.11) | collective-permute-done | bytes 524320 | tf_op jit(solution)/shard_map/cond/branch_0_fun/ppermute | solution.py:643
  187.0 2.9 %collective-permute-start.13 = (bf16[8,256,128]{2,1,0:T(8,128)(2,1)}, bf16[8,256,128]{2,1,0:T(8,128)(2,1)S(1)}, u32[]{:S(2)}, u32[]{:S(2)}) collective-permute-start(bf16[8,256,128]{2,1,0:T(8,128)(2,1)} %get-tuple-element.271), channel_id=1, source_target_pairs={{0,28},{4,16},{8,20},{12,24},{16,12},{20,0},{24,4},{28,8},{1,29},{... | collective-permute-start | bytes 1572872 | tf_op jit(solution)/shard_map/cond/branch_0_fun/ppermute | solution.py:643
  189.9 1.1 pad_maximum_fusion.refs_1_
  191.0 16.7 %finish.3 = (bf16[512,4096]{1,0:T(8,128)(2,1)}, s32[1]{0:T(128)}) custom-call(s32[2]{0:T(128)} %pad_add_fusion.nv_ref, bf16[512,4096]{1,0:T(8,128)(2,1)} %get-tuple-element.250.part_ref, bf16[512,4096]{1,0:T(8,128)(2,1)} %bitcast.199, bf16[512,128]{1,0:T(8,128)(2,1)} %get-tuple-element.252.read_ref, f32[512,128]{1,0:T(8,128)} %get-tuple-element.253.ecum_ref, ...), custom_call_target="tpu_custom_call" | custom-call | flops 1342177280 | bytes 12582912 | tf_op jit(solution)/shard_map/cond/branch_0_fun/finish/pallas_call | solution.py:246
  207.7 1.9 convert_add_fusion.final_ref
  209.6 32.4 %collective-permute-done.13.refs_7_ = bf16[8,256,128]{2,1,0:T(8,128)(2,1)S(1)} collective-permute-done((bf16[8,256,128]{2,1,0:T(8,128)(2,1)}, bf16[8,256,128]{2,1,0:T(8,128)(2,1)S(1)}, u32[]{:S(2)}, u32[]{:S(2)}) %collective-permute-start.13) | collective-permute-done | bytes 524320 | tf_op jit(solution)/shard_map/cond/branch_0_fun/ppermute | solution.py:643
  243.1 5.0 %land.3 = f32[13,1024,128]{2,1,0:T(8,128)} custom-call(s32[3,13]{1,0:T(4,128)S(1)} %copy-done.36, f32[128,1024]{1,0:T(8,128)} %convert_add_fusion.final_ref, f32[1,1024]{1,0:T(1,128)} %bitcast.237, bf16[1024,128]{1,0:T(8,128)(2,1)} %bitcast.220, bf16[8,256,128]{2,1,0:T(8,128)(2,1)} %copy-done.12, bf16[12,256,128]{2,1,0:T(8,128)(2,1)} %get-tuple-element.264.refs_0_, ...), custom_call_target="tpu_custom_call" | custom-call | flops 34078720 | bytes 10223616 | tf_op jit(solution)/shard_map/cond/branch_0_fun/land/pallas_call | solution.py:576
  (130 shorter events, 26.9 us)
Async XLA Ops:
  5.2 16.9 %all-to-all-start.3 = ((bf16[8,16,1152]{2,1,0:T(8,128)(2,1)}), bf16[8,16,1152]{2,1,0:T(8,128)(2,1)S(1)}, u32[]{:S(2)}, u32[]{:S(2)}) async-start(bf16[8,16,1152]{2,1,0:T(8,128)(2,1)} %letters.1), calls=%async_computation.3 | async-start | bytes 589824 | tf_op jit(solution)/shard_map/all_to_all | solution.py:595
  16.0 5.5 %copy-start.42 = (f32[64]{0:T(128)S(1)}, f32[64]{0:T(128)}, u32[]{:S(2)}) copy-start(f32[64]{0:T(128)} %param.37) | copy-start | bytes 772
  22.1 0.7 copy-start
  22.8 42.3 %all-to-all-start.4 = ((bf16[4,13,256,128]{3,2,1,0:T(8,128)(2,1)}), bf16[4,13,256,128]{3,2,1,0:T(8,128)(2,1)S(1)}, u32[]{:S(2)}, u32[]{:S(2)}) async-start(bf16[4,13,256,128]{3,2,1,0:T(8,128)(2,1)} %pack.1), calls=%async_computation.4 | async-start | bytes 6815744 | tf_op jit(solution)/shard_map/all_to_all | solution.py:636
  31.6 14.4 %copy-start.32 = (s32[8,39]{1,0:T(8,128)}, s32[8,39]{1,0:T(8,128)S(1)}, u32[]{:S(2)}) copy-start(s32[8,39]{1,0:T(8,128)S(1)} %fusion.14.plan_ref) | copy-start | bytes 3748
  44.6 0.7 copy-start.28
  75.0 9.2 %copy-start.43 = (f32[64]{0:T(128)S(1)}, f32[64]{0:T(128)}, u32[]{:S(2)}) copy-start(f32[64]{0:T(128)} %get-tuple-element.248) | copy-start | bytes 772 | tf_op jit(solution)/shard_map/cond
  75.0 9.2 %copy-start.46 = (f32[64]{0:T(128)S(1)}, f32[64]{0:T(128)}, u32[]{:S(2)}) copy-start(f32[64]{0:T(128)} %get-tuple-element.249) | copy-start | bytes 772 | tf_op jit(solution)/shard_map/cond
  75.0 9.8 %copy-start.16 = (f32[3,4352]{1,0:T(4,128)S(1)}, f32[3,4352]{1,0:T(4,128)}, u32[]{:S(2)}) copy-start(f32[3,4352]{1,0:T(4,128)} %get-tuple-element.242) | copy-start | bytes 156676 | tf_op jit(solution)/shard_map/cond
  85.4 36.1 %copy-start.1 = (bf16[8,16,1152]{2,1,0:T(8,128)(2,1)S(1)}, bf16[8,16,1152]{2,1,0:T(8,128)(2,1)}, u32[]{:S(2)}) copy-start(bf16[8,16,1152]{2,1,0:T(8,128)(2,1)} %get-tuple-element.261) | copy-start | bytes 884740 | tf_op jit(solution)/shard_map/cond
  110.6 22.5 %collective-permute-start.2 = (bf16[128,4096]{1,0:T(8,128)(2,1)}, bf16[128,4096]{1,0:T(8,128)(2,1)S(1)}, u32[]{:S(2)}, u32[]{:S(2)}) collective-permute-start(bf16[128,4096]{1,0:T(8,128)(2,1)} %get-tuple-element.259), channel_id=1, source_target_pairs={{0,1},{1,0},{2,3},{3,2},{4,5},{5,4},{6,7},{7,6},{8,9},{9,8},{10,11... | collective-permute-start | bytes 3145736 | tf_op jit(solution)/shard_map/cond/branch_0_fun/ppermute | solution.py:599
  110.7 20.8 %all-to-all-start = ((bf16[8,256,128]{2,1,0:T(8,128)(2,1)}), bf16[8,256,128]{2,1,0:T(8,128)(2,1)S(1)}, u32[]{:S(2)}, u32[]{:S(2)}) async-start(bf16[8,256,128]{2,1,0:T(8,128)(2,1)} %get-tuple-element.256), calls=%async_computation | async-start | bytes 1048576 | tf_op jit(solution)/shard_map/cond/branch_0_fun/all_to_all | solution.py:595
  115.5 126.5 %collective-permute-start.7 = (bf16[12,256,128]{2,1,0:T(8,128)(2,1)}, bf16[12,256,128]{2,1,0:T(8,128)(2,1)}, u32[]{:S(2)}, u32[]{:S(2)}) collective-permute-start(bf16[12,256,128]{2,1,0:T(8,128)(2,1)} %get-tuple-element.265), channel_id=1, source_target_pairs={{0,4},{4,8},{8,12},{12,0},{16,20},{20,24},{24,28},{28,16},{1,5},{5... | collective-permute-start | bytes 2359304 | tf_op jit(solution)/shard_map/cond/branch_0_fun/ppermute | solution.py:643
  117.5 124.5 %collective-permute-start.8 = (bf16[12,256,128]{2,1,0:T(8,128)(2,1)}, bf16[12,256,128]{2,1,0:T(8,128)(2,1)}, u32[]{:S(2)}, u32[]{:S(2)}) collective-permute-start(bf16[12,256,128]{2,1,0:T(8,128)(2,1)} %get-tuple-element.266), channel_id=1, source_target_pairs={{0,8},{4,12},{8,0},{12,4},{16,24},{20,28},{24,16},{28,20},{1,9},{5... | collective-permute-start | bytes 2359304 | tf_op jit(solution)/shard_map/cond/branch_0_fun/ppermute | solution.py:643
  119.0 45.5 %collective-permute-start.10 = (bf16[8,256,128]{2,1,0:T(8,128)(2,1)}, bf16[8,256,128]{2,1,0:T(8,128)(2,1)}, u32[]{:S(2)}, u32[]{:S(2)}) collective-permute-start(bf16[8,256,128]{2,1,0:T(8,128)(2,1)} %get-tuple-element.268), channel_id=1, source_target_pairs={{0,16},{4,20},{8,24},{12,28},{16,0},{20,4},{24,8},{28,12},{1,17},{... | collective-permute-start | bytes 1572872 | tf_op jit(solution)/shard_map/cond/branch_0_fun/ppermute | solution.py:643
  121.8 13.4 %copy-start.33 = (f32[4096]{0:T(1024)}, f32[4096]{0:T(1024)S(1)}, u32[]{:S(2)}) copy-start(f32[4096]{0:T(1024)S(1)} %broadcast_in_dim.209) | copy-start | bytes 49156 | tf_op jit(solution)/shard_map/cond
  131.5 12.1 %copy-start.12 = (bf16[8,256,128]{2,1,0:T(8,128)(2,1)}, bf16[8,256,128]{2,1,0:T(8,128)(2,1)S(1)}, u32[]{:S(2)}) copy-start(bf16[8,256,128]{2,1,0:T(8,128)(2,1)S(1)} %all-to-all-done.first_ref) | copy-start | bytes 1572868 | tf_op jit(solution)/shard_map/cond
  131.5 12.6 %copy-start.49 = (s32[13]{0:T(128)S(1)}, s32[13]{0:T(128)}, u32[]{:S(2)}) copy-start(s32[13]{0:T(128)} %get-tuple-element.262) | copy-start | bytes 160 | tf_op jit(solution)/shard_map/cond
  131.6 29.9 %copy-start.9 = (bf16[4,256,128]{2,1,0:T(8,128)(2,1)}, bf16[4,256,128]{2,1,0:T(8,128)(2,1)S(1)}, u32[]{:S(2)}) copy-start(bf16[4,256,128]{2,1,0:T(8,128)(2,1)S(1)} %dynamic-slice_select_fusion) | copy-start | bytes 786436 | tf_op jit(solution)/shard_map/cond
  131.6 18.7 %collective-permute-start = (bf16[1,1024,128]{2,1,0:T(8,128)(2,1)S(1)}, bf16[1,1024,128]{2,1,0:T(8,128)(2,1)S(1)}, u32[]{:S(2)}, u32[]{:S(2)}) collective-permute-start(bf16[1,1024,128]{2,1,0:T(8,128)(2,1)S(1)} %bitcast.217), channel_id=1, source_target_pairs={{0,2},{1,3},{2,0},{3,1},{4,6},{5,7},{6,4},{7,5},{8,10},{9,11},{10,... | collective-permute-start | bytes 786440 | tf_op jit(solution)/shard_map/cond/branch_0_fun/ppermute | solution.py:599
  133.2 12.2 %copy-start.5 = (bf16[128,4096]{1,0:T(8,128)(2,1)}, bf16[128,4096]{1,0:T(8,128)(2,1)S(1)}, u32[]{:S(2)}) copy-start(bf16[128,4096]{1,0:T(8,128)(2,1)S(1)} %collective-permute-done.2.refs_0_) | copy-start | bytes 3145732 | tf_op jit(solution)/shard_map/cond
  135.2 26.2 %copy-start.13 = (bf16[128,4096]{1,0:T(8,128)(2,1)}, bf16[128,4096]{1,0:T(8,128)(2,1)S(1)}, u32[]{:S(2)}) copy-start(bf16[128,4096]{1,0:T(8,128)(2,1)S(1)} %add_convert_fusion) | copy-start | bytes 3145732 | tf_op jit(solution)/shard_map/cond
  137.1 8.2 %copy-start.39 = (pred[3]{0:T(512)(128)(4,1)}, pred[3]{0:T(512)(128)(4,1)S(1)}, u32[]{:S(2)}) copy-start(pred[3]{0:T(512)(128)(4,1)S(1)} %get-tuple-element.553) | copy-start | bytes 13 | tf_op jit(solution)/shard_map/cond
  142.0 3.3 %copy-start.52 = (pred[3]{0:T(512)(128)(4,1)}, pred[3]{0:T(512)(128)(4,1)S(1)}, u32[]{:S(2)}) copy-start(pred[3]{0:T(512)(128)(4,1)S(1)} %compare_and_fusion.2) | copy-start | bytes 13 | tf_op jit(solution)/shard_map/cond
  143.6 4.3 %collective-permute-start.5 = (bf16[1,3,4352]{2,1,0:T(4,128)(2,1)}, bf16[1,3,4352]{2,1,0:T(4,128)(2,1)}, u32[]{:S(2)}, u32[]{:S(2)}) collective-permute-start(bf16[1,3,4352]{2,1,0:T(4,128)(2,1)} %maximum_select_fusion.1), channel_id=1, source_target_pairs={{0,2},{1,3},{2,0},{3,1},{4,6},{5,7},{6,4},{7,5},{8,10},{9,11},{10,... | collective-permute-start | bytes 78344 | tf_op jit(solution)/shard_map/cond/branch_0_fun/ppermute | solution.py:599
  146.2 14.9 %copy-start.56 = (bf16[8,256,128]{2,1,0:T(8,128)(2,1)S(1)}, bf16[8,256,128]{2,1,0:T(8,128)(2,1)}, u32[]{:S(2)}) copy-start(bf16[8,256,128]{2,1,0:T(8,128)(2,1)} %get-tuple-element.269) | copy-start | bytes 1572868 | tf_op jit(solution)/shard_map/cond
  147.9 11.9 %collective-permute-start.3 = (bf16[128,2048]{1,0:T(8,128)(2,1)S(1)}, bf16[128,2048]{1,0:T(8,128)(2,1)S(1)}, u32[]{:S(2)}, u32[]{:S(2)}) collective-permute-start(bf16[128,2048]{1,0:T(8,128)(2,1)S(1)} %constant_dynamic-slice_fusion.1), channel_id=1, source_target_pairs={{0,2},{1,3},{2,0},{3,1},{4,6},{5,7},{6,4},{7,5},{8,10},{9,11},{10,... | collective-permute-start | bytes 1572872 | tf_op jit(solution)/shard_map/cond/branch_0_fun/ppermute | solution.py:599
  150.2 1.3 collective-permute-start.6
  151.6 9.5 %collective-permute-start.1 = (bf16[2,1024,128]{2,1,0:T(8,128)(2,1)S(1)}, bf16[2,1024,128]{2,1,0:T(8,128)(2,1)S(1)}, u32[]{:S(2)}, u32[]{:S(2)}) collective-permute-start(bf16[2,1024,128]{2,1,0:T(8,128)(2,1)S(1)} %pad_maximum_fusion.2), channel_id=1, source_target_pairs={{0,1},{1,0},{2,3},{3,2},{4,5},{5,4},{6,7},{7,6},{8,9},{9,8},{10,11... | collective-permute-start | bytes 1572872 | tf_op jit(solution)/shard_map/cond/branch_0_fun/ppermute | solution.py:599
  159.7 2.8 %collective-permute-start.4 = (bf16[128,2048]{1,0:T(8,128)(2,1)S(1)}, bf16[128,2048]{1,0:T(8,128)(2,1)S(1)}, u32[]{:S(2)}, u32[]{:S(2)}) collective-permute-start(bf16[128,2048]{1,0:T(8,128)(2,1)S(1)} %collective-permute-done.3), channel_id=1, source_target_pairs={{0,1},{1,0},{2,3},{3,2},{4,5},{5,4},{6,7},{7,6},{8,9},{9,8},{10,11... | collective-permute-start | bytes 1572872 | tf_op jit(solution)/shard_map/cond/branch_0_fun/ppermute | solution.py:599
  161.1 25.9 %collective-permute-start.11 = (bf16[8,256,128]{2,1,0:T(8,128)(2,1)S(1)}, bf16[8,256,128]{2,1,0:T(8,128)(2,1)}, u32[]{:S(2)}, u32[]{:S(2)}) collective-permute-start(bf16[8,256,128]{2,1,0:T(8,128)(2,1)S(1)} %copy-done.56), channel_id=1, source_target_pairs={{0,20},{4,24},{8,28},{12,16},{16,4},{20,8},{24,12},{28,0},{1,21},{... | collective-permute-start | bytes 1572872 | tf_op jit(solution)/shard_map/cond/branch_0_fun/ppermute | solution.py:643
  162.6 28.4 %copy-start.29 = (f32[4096]{0:T(1024)S(1)}, f32[4096]{0:T(1024)}, u32[]{:S(2)}) copy-start(f32[4096]{0:T(1024)} %get-tuple-element.258) | copy-start | bytes 49156 | tf_op jit(solution)/shard_map/cond
  162.6 79.5 %collective-permute-start.9 = (bf16[12,256,128]{2,1,0:T(8,128)(2,1)}, bf16[12,256,128]{2,1,0:T(8,128)(2,1)S(1)}, u32[]{:S(2)}, u32[]{:S(2)}) collective-permute-start(bf16[12,256,128]{2,1,0:T(8,128)(2,1)} %get-tuple-element.267), channel_id=1, source_target_pairs={{0,12},{4,0},{8,4},{12,8},{16,28},{20,16},{24,20},{28,24},{1,13},{... | collective-permute-start | bytes 2359304 | tf_op jit(solution)/shard_map/cond/branch_0_fun/ppermute | solution.py:643
  164.5 45.1 %collective-permute-start.12 = (bf16[8,256,128]{2,1,0:T(8,128)(2,1)}, bf16[8,256,128]{2,1,0:T(8,128)(2,1)S(1)}, u32[]{:S(2)}, u32[]{:S(2)}) collective-permute-start(bf16[8,256,128]{2,1,0:T(8,128)(2,1)} %get-tuple-element.270), channel_id=1, source_target_pairs={{0,24},{4,28},{8,16},{12,20},{16,8},{20,12},{24,0},{28,4},{1,25},{... | collective-permute-start | bytes 1572872 | tf_op jit(solution)/shard_map/cond/branch_0_fun/ppermute | solution.py:643
  187.0 55.1 %collective-permute-start.13 = (bf16[8,256,128]{2,1,0:T(8,128)(2,1)}, bf16[8,256,128]{2,1,0:T(8,128)(2,1)S(1)}, u32[]{:S(2)}, u32[]{:S(2)}) collective-permute-start(bf16[8,256,128]{2,1,0:T(8,128)(2,1)} %get-tuple-element.271), channel_id=1, source_target_pairs={{0,28},{4,16},{8,20},{12,24},{16,12},{20,0},{24,4},{28,8},{1,29},{... | collective-permute-start | bytes 1572872 | tf_op jit(solution)/shard_map/cond/branch_0_fun/ppermute | solution.py:643
  191.0 16.7 %dynamic-slice-start = ((f32[4096]{0:T(1024)}, s32[]{:T(128)}), f32[1024]{0:T(1024)S(1)}, s32[]{:S(2)}) async-start(f32[4096]{0:T(1024)} %copy-done.33, s32[]{:T(128)} %select_n.338), calls=%async_computation.5 | async-start | bytes 8704 | tf_op jit(solution)/shard_map/dynamic-slice.5
  191.0 52.1 %copy-start.36 = (s32[3,13]{1,0:T(4,128)S(1)}, s32[3,13]{1,0:T(4,128)}, u32[]{:S(2)}) copy-start(s32[3,13]{1,0:T(4,128)} %get-tuple-element.255.info_ref) | copy-start | bytes 472 | tf_op jit(solution)/shard_map/cond
  209.6 32.4 %copy-start.26 = (bf16[8,256,128]{2,1,0:T(8,128)(2,1)}, bf16[8,256,128]{2,1,0:T(8,128)(2,1)S(1)}, u32[]{:S(2)}) copy-start(bf16[8,256,128]{2,1,0:T(8,128)(2,1)S(1)} %collective-permute-done.12.refs_6_) | copy-start | bytes 1572868 | tf_op jit(solution)/shard_map/cond
  242.0 0.8 copy-start.27
  242.0 1.1 copy-start.22
